TPU v7x, 32 devices: a whole 2x2x4 slice. The times are simulated.
32 devices in a mesh: dp: 8 (over z, y), shard: 4 (over x, core).
Axes of the slice: x: 2, y: 2, z: 4, core: 2. Of those that a mesh axis runs over, the one named last changes fastest.
Arguments:
- tokens: bfloat16 [512, 4096], P('shard', 'dp'), may hold values from -6 to 6
- cotangent: bfloat16 [512, 4096], P('shard', 'dp'), may hold values from -2 to 2
- expert_ids: int32 [512, 2], P('shard'), may hold values from 0 to 7, all different within a row; in each aligned block of 128 rows (0 to 127, 128 to 255, ...) at most 56 rows name the same one
- probs: float32 [512, 2], P('shard'), may hold values from 0.1 to 1
- gate_weight: bfloat16 [8, 4096, 768], P('shard', 'dp'), may hold values from -0.09375 to 0.09375
- up_weight: bfloat16 [8, 4096, 768], P('shard', 'dp'), may hold values from -0.09375 to 0.09375
- down_weight: bfloat16 [8, 768, 4096], P('shard', None, 'dp'), may hold values from -0.21875 to 0.21875
Outputs:
- mixed: bfloat16 [512, 4096], P('shard', 'dp')
- grad_tokens: bfloat16 [512, 4096], P('shard', 'dp')
- grad_gate: bfloat16 [8, 4096, 768], P('shard', 'dp')
- grad_up: bfloat16 [8, 4096, 768], P('shard', 'dp')
- grad_down: bfloat16 [8, 768, 4096], P('shard', None, 'dp')
Inputs may be any that keep to these rules, and one draw needn't show every extreme that they name: `expert_ids`: each token names 2 different experts; among the 128 tokens of one index of shard no expert is named more than 56 times.
All inputs are finite; a program needn't handle non-finite values.
Results may differ from a plain program's by a relative error of at most 0.029.
Values may be sent and summed in bfloat16 or wider, within the bound.
No kernel may reach another device: no remote copies, remote signals or barrier semaphores. Data moves between devices by JAX's collectives and lax.ppermute only.
A program may use at most 64 MiB of HBM per device.

v0:
```python
import jax
import jax.numpy as jnp
from jax import lax
from jax.sharding import PartitionSpec as P


BF = jnp.bfloat16
F32 = jnp.float32
CUTS = 2
CROSS = ((0,1), (1,0), (0,1), (0,1), (1,0), (0,1))


def power_of_two(n):
    return n & (n - 1) == 0


def swap(x, axis, k):
    n = lax.axis_size(axis)
    return lax.ppermute(x, axis, [(i, i ^ k) for i in range(n)])


def gather_peers(x, after=None):
    n = lax.axis_size("shard")
    if not (power_of_two(n) and n <= 8):
        every = lax.all_gather(x, "shard")
        return [every[k] for k in range(n)]
    blocks = [x]
    k = n // 2
    while k >= 1:
        sent = blocks
        if after is not None and k == n // 2:
            sent = [lax.optimization_barrier((x, after))[0]]
        got = []
        for block in sent:
            got.append(swap(block, "shard", k))
        blocks = [b for pair in zip(blocks, got) for b in pair]
        k //= 2
    return blocks


def peer_place(shard):
    n = lax.axis_size("shard")
    if power_of_two(n) and n <= 8:
        return shard ^ lax.axis_index("shard")
    return shard


def exchange_peers(blocks):
    n = lax.axis_size("shard")
    if power_of_two(n) and n <= 8:
        return [blocks[0]] + [swap(blocks[k], "shard", k) for k in range(1, n)]
    got = lax.all_to_all(jnp.stack(blocks), "shard", split_axis=0, concat_axis=0, tiled=True)
    return [got[k] for k in range(n)]


def halvings(crossed):
    n = lax.axis_size("dp")
    order = []
    while 1 << (len(order) + 1) < n:
        order.append((1 << len(order), len(order)))
    if crossed and len(order) > 1:
        order[0], order[1] = order[1], order[0]
    return order


def bit_of(k):
    return (lax.axis_index("dp") // k) % 2


def sum_rows(x, crossed=False):
    n = lax.axis_size("dp")
    if not power_of_two(n):
        return lax.psum_scatter(x, "dp", scatter_dimension=0, tiled=True).astype(F32)
    order = halvings(crossed)
    x = x.reshape((2,) * len(order) + (-1, x.shape[-1]))
    gone = []
    for k, place in order:
        axis = place - sum(g < place for g in gone)
        gone.append(place)
        bit = bit_of(k)
        mine = lax.dynamic_index_in_dim(x, bit, axis, keepdims=False)
        other = lax.dynamic_index_in_dim(x, 1 - bit, axis, keepdims=False)
        got = swap(other.astype(BF), "dp", k)
        x = mine.astype(F32) + got.astype(F32)
    if n > 1:
        x = x.astype(BF)
        x = x.astype(F32) + swap(x, "dp", n // 2).astype(F32)
    return x


def gather_rows(x, crossed=False):
    n = lax.axis_size("dp")
    if not power_of_two(n):
        return lax.all_gather(x, "dp", axis=0, tiled=True)
    units = x.shape[-1]
    here = []
    for k, place in reversed(halvings(crossed)):
        axis = sum(h < place for h in here)
        here.append(place)
        got = swap(x, "dp", k)
        x = jnp.where(bit_of(k) == 1, jnp.stack((got, x), axis), jnp.stack((x, got), axis))
    return x.reshape(-1, units)


def mm(form, a, b):
    return jnp.einsum(form, a, b, preferred_element_type=F32)


def local(tokens, cotangent, expert_ids, probs, gate_weight, up_weight, down_weight):
    token_count, slice_width = tokens.shape
    top = expert_ids.shape[1]
    held = gate_weight.shape[0]
    units = gate_weight.shape[2]
    shards = lax.axis_size("shard")
    experts = held * shards
    me = lax.axis_index("shard")
    capacity = 2 * max(1, 7 * token_count * top // (8 * experts))
    rows = shards * capacity

    meta = jnp.concatenate((expert_ids.T.astype(F32), probs.T), axis=0)
    token_blocks = gather_peers(tokens)
    metas = jnp.stack(gather_peers(meta))
    cot_blocks = gather_peers(cotangent, token_blocks[shards // 2])

    earlier = (
        jnp.arange(token_count)[:, None] < jnp.arange(token_count)[None, :]
    ).astype(BF)

    ids_in = metas[:, :top, :].astype(jnp.int32)
    probs_in = metas[:, top:, :]
    mine = (me * held + jnp.arange(held))[:, None, None, None]
    named = ids_in[None] == mine
    hit = jnp.any(named, axis=2)
    weight_of = jnp.sum(jnp.where(named, probs_in[None], 0.0), axis=2)
    place = mm("jst,tu->jsu", hit.astype(BF), earlier).astype(jnp.int32)
    slots = jnp.arange(capacity)[None, None, :, None]
    chosen = hit[:, :, None, :] & (place[:, :, None, :] == slots)
    pick = chosen.astype(BF)
    slot_prob = jnp.sum(jnp.where(chosen, weight_of[:, :, None, :], 0.0), axis=3)

    rows_in = jnp.stack(
        [mm("jct,td->jcd", pick[:, k], token_blocks[k]).astype(BF) for k in range(shards)], axis=1
    )
    grad_out = jnp.stack(
        [
            (slot_prob[:, k, :, None] * mm("jct,td->jcd", pick[:, k], cot_blocks[k])).astype(BF)
            for k in range(shards)
        ],
        axis=1,
    ).reshape(held, rows, slice_width)
    rows_in = rows_in.reshape(held, rows, slice_width)
    gate_part = mm("jrd,jdf->jrf", rows_in, gate_weight).astype(BF).reshape(held * rows, units)
    up_part = mm("jrd,jdf->jrf", rows_in, up_weight).astype(BF).reshape(held * rows, units)
    grad_part = mm("jrd,jfd->jrf", grad_out, down_weight).astype(BF).reshape(held * rows, units)

    cuts = CUTS if units % (128 * CUTS) == 0 else 1
    wide = units // cuts
    hidden, gg, gu = [], [], []
    for cut in range(cuts):
        part = slice(cut * wide, (cut + 1) * wide)
        gate = sum_rows(gate_part[:, part], CROSS[0][cut])
        upward = sum_rows(up_part[:, part], CROSS[1][cut])
        grad_hidden = sum_rows(grad_part[:, part], CROSS[2][cut])
        sigmoid_gate = jax.nn.sigmoid(gate)
        activated = gate * sigmoid_gate
        hidden.append(gather_rows((activated * upward).astype(BF), CROSS[3][cut]))
        grad_gate_row = (
            grad_hidden * upward * sigmoid_gate * (1.0 + gate * (1.0 - sigmoid_gate))
        ).astype(BF)
        grad_up_row = (grad_hidden * activated).astype(BF)
        gg.append(gather_rows(grad_gate_row, CROSS[4][cut]))
        gu.append(gather_rows(grad_up_row, CROSS[5][cut]))
    hidden, gg, gu = (
        jnp.concatenate(x, axis=1).reshape(held, rows, units) for x in (hidden, gg, gu)
    )

    expert_out = mm("jrf,jfd->jrd", hidden, down_weight).astype(BF)
    expert_out = expert_out.reshape(held, shards, capacity, slice_width)
    returned = exchange_peers([expert_out[:, k] for k in range(shards)])
    grad_down = mm("jrf,jrd->jfd", hidden, grad_out).astype(BF)

    grad_row = (
        mm("jrf,jdf->jrd", gg, gate_weight) + mm("jrf,jdf->jrd", gu, up_weight)
    ).astype(BF)
    gg, gu, grad_row = lax.optimization_barrier((gg, gu, grad_row))
    grad_row = grad_row.reshape(held, shards, capacity, slice_width)
    grad_back = exchange_peers([grad_row[:, k] for k in range(shards)])
    grad_gate = mm("jrd,jrf->jdf", rows_in, gg).astype(BF)
    grad_up = mm("jrd,jrf->jdf", rows_in, gu).astype(BF)

    home = expert_ids.T[None] == jnp.arange(experts)[:, None, None]
    home_hit = jnp.any(home, axis=1)
    home_place = mm("et,tu->eu", home_hit.astype(BF), earlier).astype(jnp.int32)
    spot = jnp.sum(jnp.where(home, home_place[:, None, :], 0), axis=0)
    owner = expert_ids.T // held
    slot = (peer_place(owner) * held + expert_ids.T % held) * capacity + spot
    back = (slot[:, :, None] == jnp.arange(experts * capacity)).astype(BF)
    out_rows = jnp.concatenate(returned).reshape(experts * capacity, slice_width)
    grad_rows = jnp.concatenate(grad_back).reshape(experts * capacity, slice_width)
    out_pairs = mm("ktr,rd->ktd", back, out_rows)
    mixed = jnp.sum(probs.T[:, :, None] * out_pairs, axis=0).astype(BF)
    grad_tokens = mm("tr,rd->td", jnp.sum(back, axis=0), grad_rows).astype(BF)
    return (mixed, grad_tokens, grad_gate, grad_up, grad_down)


def solution(mesh):
    placed = (
        P("shard", "dp"),
        P("shard", "dp"),
        P("shard", None),
        P("shard", None),
        P("shard", "dp", None),
        P("shard", "dp", None),
        P("shard", None, "dp"),
    )
    return jax.shard_map(
        local,
        mesh=mesh,
        in_specs=placed,
        out_specs=(
            P("shard", "dp"),
            P("shard", "dp"),
            P("shard", "dp", None),
            P("shard", "dp", None),
            P("shard", None, "dp"),
        ),
        check_vma=False,
    )
```

profile of v0, /device:TPU:0, one launch (start us, length us, event | category | flops | bytes accessed | tf_op | source)
XLA Modules:
  0.0 94.1 jit_solution(2096342085588604631)
XLA Ops:
  0.6 0.8 bitcast_convert_fusion
  1.4 0.7 pad_maximum_fusion.10
  2.1 3.0 %collective-permute-start.1 = (f32[4,128]{1,0:T(4,128)S(1)}, f32[4,128]{1,0:T(4,128)S(1)}, u32[]{:S(2)}, u32[]{:S(2)}) collective-permute-start(f32[4,128]{1,0:T(4,128)S(1)} %pad_maximum_fusion.10), channel_id=1, source_target_pairs={{0,2},{1,3},{2,0},{3,1},{4,6},{5,7},{6,4},{7,5},{8,10},{9,11},{10,... | collective-permute-start | bytes 6152 | tf_op jit(solution)/shard_map/ppermute | solution.py:19
  6.6 0.7 select_reduce_fusion.1
  7.3 0.7 multiply_add_fusion
  8.5 0.8 collective-permute-done.2
  9.9 1.1 %fusion.9 = bf16[2,1,56,512]{3,2,0,1:T(8,128)(2,1)S(1)} fusion(bf16[128,512]{1,0:T(8,128)(2,1)} %param.8, f32[2,56]{1,0:T(2,128)S(1)} %get-tuple-element.35, pred[2,4,56,128]{3,2,0,1:T(8,128)(4,1)S(1)} %fusion.17), kind=kOutput, calls=%fused_computation.27 | convolution fusion | flops 14794752 | bytes 261120 | tf_op jit(solution)/shard_map/jct,td->jcd/dot_general | solution.py:106
  11.0 1.2 %fusion.10 = bf16[2,1,56,512]{3,2,0,1:T(8,128)(2,1)S(1)} fusion(bf16[128,512]{1,0:T(8,128)(2,1)} %param.7, pred[2,4,56,128]{3,2,0,1:T(8,128)(4,1)S(1)} %fusion.17), kind=kOutput, calls=%fused_computation.28 | convolution fusion | flops 14737408 | bytes 260096 | tf_op jit(solution)/shard_map/jct,td->jcd/dot_general | solution.py:106
  12.2 1.9 %collective-permute-start.26 = (bf16[128,512]{1,0:T(8,128)(2,1)}, bf16[128,512]{1,0:T(8,128)(2,1)S(1)}, u32[]{:S(2)}, u32[]{:S(2)}) collective-permute-start(bf16[128,512]{1,0:T(8,128)(2,1)} %param.8), channel_id=1, source_target_pairs={{0,2},{1,3},{2,0},{3,1},{4,6},{5,7},{6,4},{7,5},{8,10},{9,11},{10,... | collective-permute-start | bytes 393224 | tf_op jit(solution)/shard_map/ppermute | solution.py:19
  14.7 1.0 %collective-permute-done.5 = bf16[128,512]{1,0:T(8,128)(2,1)S(1)} collective-permute-done((bf16[128,512]{1,0:T(8,128)(2,1)S(1)}, bf16[128,512]{1,0:T(8,128)(2,1)S(1)}, u32[]{:S(2)}, u32[]{:S(2)}) %collective-permute-start.5) | collective-permute-done | bytes 131104 | tf_op jit(solution)/shard_map/ppermute | solution.py:19
  16.6 1.6 %collective-permute-start.9 = (bf16[2,112,384]{2,1,0:T(8,128)(2,1)S(1)}, bf16[2,112,384]{2,1,0:T(8,128)(2,1)S(1)}, u32[]{:S(2)}, u32[]{:S(2)}) collective-permute-start(bf16[2,112,384]{2,1,0:T(8,128)(2,1)S(1)} %dynamic-slice_bitcast_fusion.4), channel_id=1, source_target_pairs={{0,8},{4,12},{8,0},{12,4},{16,24},{20,28},{24,16},{28,20},{1,9},{5... | collective-permute-start | bytes 516104 | tf_op jit(solution)/shard_map/ppermute | solution.py:19
  18.3 1.6 %collective-permute-start.17 = (bf16[2,112,384]{2,1,0:T(8,128)(2,1)S(1)}, bf16[2,112,384]{2,1,0:T(8,128)(2,1)S(1)}, u32[]{:S(2)}, u32[]{:S(2)}) collective-permute-start(bf16[2,112,384]{2,1,0:T(8,128)(2,1)S(1)} %dynamic-slice_bitcast_fusion.2), channel_id=1, source_target_pairs={{0,4},{4,0},{8,12},{12,8},{16,20},{20,16},{24,28},{28,24},{1,5},{5... | collective-permute-start | bytes 516104 | tf_op jit(solution)/shard_map/ppermute | solution.py:19
  21.2 0.7 collective-permute-start.14
  23.2 1.3 %collective-permute-start.28 = (bf16[2,112,384]{2,1,0:T(8,128)(2,1)S(1)}, bf16[2,112,384]{2,1,0:T(8,128)(2,1)S(1)}, u32[]{:S(2)}, u32[]{:S(2)}) collective-permute-start(bf16[2,112,384]{2,1,0:T(8,128)(2,1)S(1)} %dynamic-slice_bitcast_fusion.1), channel_id=1, source_target_pairs={{0,4},{4,0},{8,12},{12,8},{16,20},{20,16},{24,28},{28,24},{1,5},{5... | collective-permute-start | bytes 516104 | tf_op jit(solution)/shard_map/ppermute | solution.py:19
  24.5 1.6 %collective-permute-start.33 = (bf16[2,112,384]{2,1,0:T(8,128)(2,1)S(1)}, bf16[2,112,384]{2,1,0:T(8,128)(2,1)S(1)}, u32[]{:S(2)}, u32[]{:S(2)}) collective-permute-start(bf16[2,112,384]{2,1,0:T(8,128)(2,1)S(1)} %dynamic-slice_bitcast_fusion), channel_id=1, source_target_pairs={{0,8},{4,12},{8,0},{12,4},{16,24},{20,28},{24,16},{28,20},{1,9},{5... | collective-permute-start | bytes 516104 | tf_op jit(solution)/shard_map/ppermute | solution.py:19
  26.2 0.9 collective-permute-start.10
  27.2 1.7 %collective-permute-done.6 = bf16[2,112,384]{2,1,0:T(8,128)(2,1)S(1)} collective-permute-done((bf16[2,112,384]{2,1,0:T(8,128)(2,1)S(1)}, bf16[2,112,384]{2,1,0:T(8,128)(2,1)S(1)}, u32[]{:S(2)}, u32[]{:S(2)}) %collective-permute-start.6) | collective-permute-done | bytes 172064 | tf_op jit(solution)/shard_map/ppermute | solution.py:19
  29.4 1.6 %collective-permute-start.7 = (bf16[112,384]{1,0:T(8,128)(2,1)S(1)}, bf16[112,384]{1,0:T(8,128)(2,1)S(1)}, u32[]{:S(2)}, u32[]{:S(2)}) collective-permute-start(bf16[112,384]{1,0:T(8,128)(2,1)S(1)} %fusion.34), channel_id=1, source_target_pairs={{0,8},{4,12},{8,0},{12,4},{16,24},{20,28},{24,16},{28,20},{1,9},{5... | collective-permute-start | bytes 258056 | tf_op jit(solution)/shard_map/ppermute | solution.py:19
  31.2 2.6 %collective-permute-done.10 = bf16[112,384]{1,0:T(8,128)(2,1)S(1)} collective-permute-done((bf16[112,384]{1,0:T(8,128)(2,1)S(1)}, bf16[112,384]{1,0:T(8,128)(2,1)S(1)}, u32[]{:S(2)}, u32[]{:S(2)}) %collective-permute-start.10) | collective-permute-done | bytes 86048 | tf_op jit(solution)/shard_map/ppermute | solution.py:19
  33.7 1.5 %collective-permute-start.15 = (bf16[112,384]{1,0:T(8,128)(2,1)S(1)}, bf16[112,384]{1,0:T(8,128)(2,1)S(1)}, u32[]{:S(2)}, u32[]{:S(2)}) collective-permute-start(bf16[112,384]{1,0:T(8,128)(2,1)S(1)} %fusion.36), channel_id=1, source_target_pairs={{0,4},{4,0},{8,12},{12,8},{16,20},{20,16},{24,28},{28,24},{1,5},{5... | collective-permute-start | bytes 258056 | tf_op jit(solution)/shard_map/ppermute | solution.py:19
  35.3 2.7 %collective-permute-start.11 = (bf16[112,384]{1,0:T(8,128)(2,1)S(1)}, bf16[112,384]{1,0:T(8,128)(2,1)S(1)}, u32[]{:S(2)}, u32[]{:S(2)}) collective-permute-start(bf16[112,384]{1,0:T(8,128)(2,1)S(1)} %fusion.22), channel_id=1, source_target_pairs={{0,16},{4,20},{8,24},{12,28},{16,0},{20,4},{24,8},{28,12},{1,17},{... | collective-permute-start | bytes 258056 | tf_op jit(solution)/shard_map/ppermute | solution.py:19
  38.4 2.7 %collective-permute-start.8 = (bf16[112,384]{1,0:T(8,128)(2,1)S(1)}, bf16[112,384]{1,0:T(8,128)(2,1)S(1)}, u32[]{:S(2)}, u32[]{:S(2)}) collective-permute-start(bf16[112,384]{1,0:T(8,128)(2,1)S(1)} %fusion.23), channel_id=1, source_target_pairs={{0,16},{4,20},{8,24},{12,28},{16,0},{20,4},{24,8},{28,12},{1,17},{... | collective-permute-start | bytes 258056 | tf_op jit(solution)/shard_map/ppermute | solution.py:19
  42.2 4.5 %collective-permute-done.29 = bf16[112,384]{1,0:T(8,128)(2,1)S(1)} collective-permute-done((bf16[112,384]{1,0:T(8,128)(2,1)S(1)}, bf16[112,384]{1,0:T(8,128)(2,1)S(1)}, u32[]{:S(2)}, u32[]{:S(2)}) %collective-permute-start.29) | collective-permute-done | bytes 86048 | tf_op jit(solution)/shard_map/ppermute | solution.py:19
  46.7 1.0 %collective-permute-start.34 = (bf16[112,384]{1,0:T(8,128)(2,1)S(1)}, bf16[112,384]{1,0:T(8,128)(2,1)S(1)}, u32[]{:S(2)}, u32[]{:S(2)}) collective-permute-start(bf16[112,384]{1,0:T(8,128)(2,1)S(1)} %fusion.39), channel_id=1, source_target_pairs={{0,4},{4,0},{8,12},{12,8},{16,20},{20,16},{24,28},{28,24},{1,5},{5... | collective-permute-start | bytes 258056 | tf_op jit(solution)/shard_map/ppermute | solution.py:19
  47.7 3.4 %collective-permute-done.34 = bf16[112,384]{1,0:T(8,128)(2,1)S(1)} collective-permute-done((bf16[112,384]{1,0:T(8,128)(2,1)S(1)}, bf16[112,384]{1,0:T(8,128)(2,1)S(1)}, u32[]{:S(2)}, u32[]{:S(2)}) %collective-permute-start.34) | collective-permute-done | bytes 86048 | tf_op jit(solution)/shard_map/ppermute | solution.py:19
  51.2 2.0 %collective-permute-start.30 = (bf16[112,384]{1,0:T(8,128)(2,1)S(1)}, bf16[112,384]{1,0:T(8,128)(2,1)S(1)}, u32[]{:S(2)}, u32[]{:S(2)}) collective-permute-start(bf16[112,384]{1,0:T(8,128)(2,1)S(1)} %fusion.19), channel_id=1, source_target_pairs={{0,16},{4,20},{8,24},{12,28},{16,0},{20,4},{24,8},{28,12},{1,17},{... | collective-permute-start | bytes 258056 | tf_op jit(solution)/shard_map/ppermute | solution.py:19
  53.2 1.0 %collective-permute-start.35 = (bf16[112,384]{1,0:T(8,128)(2,1)S(1)}, bf16[112,384]{1,0:T(8,128)(2,1)S(1)}, u32[]{:S(2)}, u32[]{:S(2)}) collective-permute-start(bf16[112,384]{1,0:T(8,128)(2,1)S(1)} %fusion.18), channel_id=1, source_target_pairs={{0,16},{4,20},{8,24},{12,28},{16,0},{20,4},{24,8},{28,12},{1,17},{... | collective-permute-start | bytes 258056 | tf_op jit(solution)/shard_map/ppermute | solution.py:19
  54.2 3.2 %collective-permute-done.30 = bf16[112,384]{1,0:T(8,128)(2,1)S(1)} collective-permute-done((bf16[112,384]{1,0:T(8,128)(2,1)S(1)}, bf16[112,384]{1,0:T(8,128)(2,1)S(1)}, u32[]{:S(2)}, u32[]{:S(2)}) %collective-permute-start.30) | collective-permute-done | bytes 86048 | tf_op jit(solution)/shard_map/ppermute | solution.py:19
  57.6 1.5 %collective-permute-start.38 = (bf16[112,384]{1,0:T(8,128)(2,1)S(1)}, bf16[112,384]{1,0:T(8,128)(2,1)S(1)}, u32[]{:S(2)}, u32[]{:S(2)}) collective-permute-start(bf16[112,384]{1,0:T(8,128)(2,1)S(1)} %get-tuple-element.27), channel_id=1, source_target_pairs={{0,8},{4,12},{8,0},{12,4},{16,24},{20,28},{24,16},{28,20},{1,9},{5... | collective-permute-start | bytes 258056 | tf_op jit(solution)/shard_map/ppermute | solution.py:19
  60.3 1.6 %collective-permute-start.40 = (bf16[112,384]{1,0:T(8,128)(2,1)S(1)}, bf16[112,384]{1,0:T(8,128)(2,1)S(1)}, u32[]{:S(2)}, u32[]{:S(2)}) collective-permute-start(bf16[112,384]{1,0:T(8,128)(2,1)S(1)} %get-tuple-element.30), channel_id=1, source_target_pairs={{0,4},{4,0},{8,12},{12,8},{16,20},{20,16},{24,28},{28,24},{1,5},{5... | collective-permute-start | bytes 258056 | tf_op jit(solution)/shard_map/ppermute | solution.py:19
  61.9 1.4 %collective-permute-start.36 = (bf16[112,384]{1,0:T(8,128)(2,1)S(1)}, bf16[112,384]{1,0:T(8,128)(2,1)S(1)}, u32[]{:S(2)}, u32[]{:S(2)}) collective-permute-start(bf16[112,384]{1,0:T(8,128)(2,1)S(1)} %get-tuple-element.31), channel_id=1, source_target_pairs={{0,8},{4,12},{8,0},{12,4},{16,24},{20,28},{24,16},{28,20},{1,9},{5... | collective-permute-start | bytes 258056 | tf_op jit(solution)/shard_map/ppermute | solution.py:19
  64.5 1.0 %collective-permute-start.39 = (bf16[2,112,384]{2,1,0:T(8,128)(2,1)S(1)}, bf16[2,112,384]{2,1,0:T(8,128)(2,1)S(1)}, u32[]{:S(2)}, u32[]{:S(2)}) collective-permute-start(bf16[2,112,384]{2,1,0:T(8,128)(2,1)S(1)} %maximum_select_fusion.14), channel_id=1, source_target_pairs={{0,4},{4,0},{8,12},{12,8},{16,20},{20,16},{24,28},{28,24},{1,5},{5... | collective-permute-start | bytes 516104 | tf_op jit(solution)/shard_map/ppermute | solution.py:19
  66.3 1.0 %collective-permute-start.13 = (bf16[2,112,384]{2,1,0:T(8,128)(2,1)S(1)}, bf16[2,112,384]{2,1,0:T(8,128)(2,1)S(1)}, u32[]{:S(2)}, u32[]{:S(2)}) collective-permute-start(bf16[2,112,384]{2,1,0:T(8,128)(2,1)S(1)} %maximum_select_fusion.6), channel_id=1, source_target_pairs={{0,4},{4,0},{8,12},{12,8},{16,20},{20,16},{24,28},{28,24},{1,5},{5... | collective-permute-start | bytes 516104 | tf_op jit(solution)/shard_map/ppermute | solution.py:19
  67.4 1.0 %collective-permute-done.20 = bf16[112,384]{1,0:T(8,128)(2,1)S(1)} collective-permute-done((bf16[112,384]{1,0:T(8,128)(2,1)S(1)}, bf16[112,384]{1,0:T(8,128)(2,1)S(1)}, u32[]{:S(2)}, u32[]{:S(2)}) %collective-permute-start.20) | collective-permute-done | bytes 86048 | tf_op jit(solution)/shard_map/ppermute | solution.py:19
  68.4 1.0 %collective-permute-start.41 = (bf16[2,112,384]{2,1,0:T(8,128)(2,1)S(1)}, bf16[2,112,384]{2,1,0:T(8,128)(2,1)S(1)}, u32[]{:S(2)}, u32[]{:S(2)}) collective-permute-start(bf16[2,112,384]{2,1,0:T(8,128)(2,1)S(1)} %maximum_select_fusion.16), channel_id=1, source_target_pairs={{0,8},{4,12},{8,0},{12,4},{16,24},{20,28},{24,16},{28,20},{1,9},{5... | collective-permute-start | bytes 516104 | tf_op jit(solution)/shard_map/ppermute | solution.py:19
  69.4 1.1 %collective-permute-start.21 = (bf16[2,112,384]{2,1,0:T(8,128)(2,1)S(1)}, bf16[2,112,384]{2,1,0:T(8,128)(2,1)S(1)}, u32[]{:S(2)}, u32[]{:S(2)}) collective-permute-start(bf16[2,112,384]{2,1,0:T(8,128)(2,1)S(1)} %maximum_select_fusion.8), channel_id=1, source_target_pairs={{0,8},{4,12},{8,0},{12,4},{16,24},{20,28},{24,16},{28,20},{1,9},{5... | collective-permute-start | bytes 516104 | tf_op jit(solution)/shard_map/ppermute | solution.py:19
  70.7 2.7 %collective-permute-done.13 = bf16[2,112,384]{2,1,0:T(8,128)(2,1)S(1)} collective-permute-done((bf16[2,112,384]{2,1,0:T(8,128)(2,1)S(1)}, bf16[2,112,384]{2,1,0:T(8,128)(2,1)S(1)}, u32[]{:S(2)}, u32[]{:S(2)}) %collective-permute-start.13) | collective-permute-done | bytes 172064 | tf_op jit(solution)/shard_map/ppermute | solution.py:19
  73.9 1.7 %collective-permute-done.21 = bf16[2,112,384]{2,1,0:T(8,128)(2,1)S(1)} collective-permute-done((bf16[2,112,384]{2,1,0:T(8,128)(2,1)S(1)}, bf16[2,112,384]{2,1,0:T(8,128)(2,1)S(1)}, u32[]{:S(2)}, u32[]{:S(2)}) %collective-permute-start.21) | collective-permute-done | bytes 172064 | tf_op jit(solution)/shard_map/ppermute | solution.py:19
  76.3 1.0 %collective-permute-start.24 = (bf16[2,56,512]{2,1,0:T(8,128)(2,1)S(1)}, bf16[2,56,512]{2,1,0:T(8,128)(2,1)S(1)}, u32[]{:S(2)}, u32[]{:S(2)}) collective-permute-start(bf16[2,56,512]{2,1,0:T(8,128)(2,1)S(1)} %get-tuple-element.25), channel_id=1, source_target_pairs={{0,3},{1,2},{2,1},{3,0},{4,7},{5,6},{6,5},{7,4},{8,11},{9,10},{10,... | collective-permute-start | bytes 344072 | tf_op jit(solution)/shard_map/ppermute | solution.py:19
  77.4 1.4 %collective-permute-done.37 = bf16[2,112,384]{2,1,0:T(8,128)(2,1)S(1)} collective-permute-done((bf16[2,112,384]{2,1,0:T(8,128)(2,1)S(1)}, bf16[2,112,384]{2,1,0:T(8,128)(2,1)S(1)}, u32[]{:S(2)}, u32[]{:S(2)}) %collective-permute-start.37) | collective-permute-done | bytes 172064 | tf_op jit(solution)/shard_map/ppermute | solution.py:19
  78.8 1.6 %collective-permute-start.23 = (bf16[2,56,512]{2,1,0:T(8,128)(2,1)S(1)}, bf16[2,56,512]{2,1,0:T(8,128)(2,1)S(1)}, u32[]{:S(2)}, u32[]{:S(2)}) collective-permute-start(bf16[2,56,512]{2,1,0:T(8,128)(2,1)S(1)} %get-tuple-element.26), channel_id=1, source_target_pairs={{0,2},{1,3},{2,0},{3,1},{4,6},{5,7},{6,4},{7,5},{8,10},{9,11},{10,... | collective-permute-start | bytes 344072 | tf_op jit(solution)/shard_map/ppermute | solution.py:19
  81.1 1.8 %convolution_convert_fusion = bf16[2,768,512]{2,1,0:T(8,128)(2,1)} fusion(bf16[2,224,512]{2,1,0:T(8,128)(2,1)S(1)} %bitcast.258, bf16[2,224,384]{2,1,0:T(8,128)(2,1)S(1)} %bitcast.281, bf16[2,224,384]{2,1,0:T(8,128)(2,1)S(1)} %maximum_select_fusion), kind=kOutput, calls=%fused_computation | convolution fusion | flops 354484224 | bytes 2719744 | tf_op jit(solution)/shard_map/jrf,jrd->jfd/dot_general | solution.py:106
  84.5 1.8 %convolution_convert_fusion.2 = bf16[2,512,768]{2,1,0:T(8,128)(2,1)} fusion(bf16[2,224,512]{2,1,0:T(8,128)(2,1)S(1)} %bitcast.255, bf16[2,224,768]{2,1,0:T(8,128)(2,1)S(1)} %pad_maximum_fusion.1), kind=kOutput, calls=%fused_computation.2 | convolution fusion | flops 353107968 | bytes 2719744 | tf_op jit(solution)/shard_map/jrd,jrf->jdf/dot_general | solution.py:106
  86.3 1.8 %convolution_convert_fusion.1 = bf16[2,512,768]{2,1,0:T(8,128)(2,1)} fusion(bf16[2,224,512]{2,1,0:T(8,128)(2,1)S(1)} %bitcast.256, bf16[2,224,768]{2,1,0:T(8,128)(2,1)S(1)} %pad_maximum_fusion.2), kind=kOutput, calls=%fused_computation.1 | convolution fusion | flops 353107968 | bytes 2719744 | tf_op jit(solution)/shard_map/jrd,jrf->jdf/dot_general | solution.py:106
  88.0 1.6 %collective-permute-start.43 = (bf16[2,56,512]{2,1,0:T(8,128)(2,1)S(1)}, bf16[2,56,512]{2,1,0:T(8,128)(2,1)S(1)}, u32[]{:S(2)}, u32[]{:S(2)}) collective-permute-start(bf16[2,56,512]{2,1,0:T(8,128)(2,1)S(1)} %get-tuple-element.22), channel_id=1, source_target_pairs={{0,2},{1,3},{2,0},{3,1},{4,6},{5,7},{6,4},{7,5},{8,10},{9,11},{10,... | collective-permute-start | bytes 344072 | tf_op jit(solution)/shard_map/ppermute | solution.py:19
  89.7 1.0 %fusion.1 = bf16[128,512]{1,0:T(8,128)(2,1)} fusion(bf16[448,512,1]{1,0,2:T(8,128)(2,1)S(1)} %bitcast.297, f32[2,128]{1,0:T(2,128)S(1)} %bitcast.324, s32[2,128]{1,0:T(2,128)S(1)} %multiply_add_fusion), kind=kOutput, calls=%fused_computation.10 | convolution fusion | flops 117751808 | bytes 591872 | tf_op jit(solution)/shard_map/ktr,rd->ktd/dot_general | solution.py:106
  90.7 2.4 %collective-permute-done.43 = bf16[2,56,512]{2,1,0:T(8,128)(2,1)S(1)} collective-permute-done((bf16[2,56,512]{2,1,0:T(8,128)(2,1)S(1)}, bf16[2,56,512]{2,1,0:T(8,128)(2,1)S(1)}, u32[]{:S(2)}, u32[]{:S(2)}) %collective-permute-start.43) | collective-permute-done | bytes 114720 | tf_op jit(solution)/shard_map/ppermute | solution.py:19
  93.2 0.9 convolution_convert_fusion.7
  (145 shorter events, 15.8 us)
Async XLA Ops:
  0.6 21.8 %copy-start = (bf16[2,768,512]{2,1,0:T(8,128)(2,1)S(1)}, bf16[2,768,512]{2,1,0:T(8,128)(2,1)}, u32[]{:S(2)}) copy-start(bf16[2,768,512]{2,1,0:T(8,128)(2,1)} %param.13) | copy-start | bytes 4718596
  2.1 5.9 %collective-permute-start.1 = (f32[4,128]{1,0:T(4,128)S(1)}, f32[4,128]{1,0:T(4,128)S(1)}, u32[]{:S(2)}, u32[]{:S(2)}) collective-permute-start(f32[4,128]{1,0:T(4,128)S(1)} %pad_maximum_fusion.10), channel_id=1, source_target_pairs={{0,2},{1,3},{2,0},{3,1},{4,6},{5,7},{6,4},{7,5},{8,10},{9,11},{10,... | collective-permute-start | bytes 6152 | tf_op jit(solution)/shard_map/ppermute | solution.py:19
  5.1 3.4 %collective-permute-start = (f32[4,128]{1,0:T(4,128)S(1)}, f32[4,128]{1,0:T(4,128)S(1)}, u32[]{:S(2)}, u32[]{:S(2)}) collective-permute-start(f32[4,128]{1,0:T(4,128)S(1)} %pad_maximum_fusion.10), channel_id=1, source_target_pairs={{0,1},{1,0},{2,3},{3,2},{4,5},{5,4},{6,7},{7,6},{8,9},{9,8},{10,11... | collective-permute-start | bytes 6152 | tf_op jit(solution)/shard_map/ppermute | solution.py:19
  5.1 7.1 %collective-permute-start.4 = (bf16[128,512]{1,0:T(8,128)(2,1)}, bf16[128,512]{1,0:T(8,128)(2,1)S(1)}, u32[]{:S(2)}, u32[]{:S(2)}) collective-permute-start(bf16[128,512]{1,0:T(8,128)(2,1)} %param.7), channel_id=1, source_target_pairs={{0,2},{1,3},{2,0},{3,1},{4,6},{5,7},{6,4},{7,5},{8,10},{9,11},{10,... | collective-permute-start | bytes 393224 | tf_op jit(solution)/shard_map/ppermute | solution.py:19
  5.2 9.1 %collective-permute-start.3 = (bf16[128,512]{1,0:T(8,128)(2,1)}, bf16[128,512]{1,0:T(8,128)(2,1)S(1)}, u32[]{:S(2)}, u32[]{:S(2)}) collective-permute-start(bf16[128,512]{1,0:T(8,128)(2,1)} %param.7), channel_id=1, source_target_pairs={{0,1},{1,0},{2,3},{3,2},{4,5},{5,4},{6,7},{7,6},{8,9},{9,8},{10,11... | collective-permute-start | bytes 393224 | tf_op jit(solution)/shard_map/ppermute | solution.py:19
  5.6 8.9 %collective-permute-start.25 = (bf16[128,512]{1,0:T(8,128)(2,1)}, bf16[128,512]{1,0:T(8,128)(2,1)S(1)}, u32[]{:S(2)}, u32[]{:S(2)}) collective-permute-start(bf16[128,512]{1,0:T(8,128)(2,1)} %param.8), channel_id=1, source_target_pairs={{0,1},{1,0},{2,3},{3,2},{4,5},{5,4},{6,7},{7,6},{8,9},{9,8},{10,11... | collective-permute-start | bytes 393224 | tf_op jit(solution)/shard_map/ppermute | solution.py:19
  8.1 1.3 %collective-permute-start.2 = (f32[4,128]{1,0:T(4,128)S(1)}, f32[4,128]{1,0:T(4,128)S(1)}, u32[]{:S(2)}, u32[]{:S(2)}) collective-permute-start(f32[4,128]{1,0:T(4,128)S(1)} %collective-permute-done.1), channel_id=1, source_target_pairs={{0,1},{1,0},{2,3},{3,2},{4,5},{5,4},{6,7},{7,6},{8,9},{9,8},{10,11... | collective-permute-start | bytes 6152 | tf_op jit(solution)/shard_map/ppermute | solution.py:19
  11.0 5.0 %copy-start.1 = (bf16[2,512,768]{2,1,0:T(8,128)(2,1)S(1)}, bf16[2,512,768]{2,1,0:T(8,128)(2,1)}, u32[]{:S(2)}) copy-start(bf16[2,512,768]{2,1,0:T(8,128)(2,1)} %param.12) | copy-start | bytes 4718596
  12.2 8.4 %collective-permute-start.26 = (bf16[128,512]{1,0:T(8,128)(2,1)}, bf16[128,512]{1,0:T(8,128)(2,1)S(1)}, u32[]{:S(2)}, u32[]{:S(2)}) collective-permute-start(bf16[128,512]{1,0:T(8,128)(2,1)} %param.8), channel_id=1, source_target_pairs={{0,2},{1,3},{2,0},{3,1},{4,6},{5,7},{6,4},{7,5},{8,10},{9,11},{10,... | collective-permute-start | bytes 393224 | tf_op jit(solution)/shard_map/ppermute | solution.py:19
  14.3 1.4 %collective-permute-start.5 = (bf16[128,512]{1,0:T(8,128)(2,1)S(1)}, bf16[128,512]{1,0:T(8,128)(2,1)S(1)}, u32[]{:S(2)}, u32[]{:S(2)}) collective-permute-start(bf16[128,512]{1,0:T(8,128)(2,1)S(1)} %collective-permute-done.4), channel_id=1, source_target_pairs={{0,1},{1,0},{2,3},{3,2},{4,5},{5,4},{6,7},{7,6},{8,9},{9,8},{10,11... | collective-permute-start | bytes 393224 | tf_op jit(solution)/shard_map/ppermute | solution.py:19
  16.6 7.9 %collective-permute-start.9 = (bf16[2,112,384]{2,1,0:T(8,128)(2,1)S(1)}, bf16[2,112,384]{2,1,0:T(8,128)(2,1)S(1)}, u32[]{:S(2)}, u32[]{:S(2)}) collective-permute-start(bf16[2,112,384]{2,1,0:T(8,128)(2,1)S(1)} %dynamic-slice_bitcast_fusion.4), channel_id=1, source_target_pairs={{0,8},{4,12},{8,0},{12,4},{16,24},{20,28},{24,16},{28,20},{1,9},{5... | collective-permute-start | bytes 516104 | tf_op jit(solution)/shard_map/ppermute | solution.py:19
  18.3 7.9 %collective-permute-start.17 = (bf16[2,112,384]{2,1,0:T(8,128)(2,1)S(1)}, bf16[2,112,384]{2,1,0:T(8,128)(2,1)S(1)}, u32[]{:S(2)}, u32[]{:S(2)}) collective-permute-start(bf16[2,112,384]{2,1,0:T(8,128)(2,1)S(1)} %dynamic-slice_bitcast_fusion.2), channel_id=1, source_target_pairs={{0,4},{4,0},{8,12},{12,8},{16,20},{20,16},{24,28},{28,24},{1,5},{5... | collective-permute-start | bytes 516104 | tf_op jit(solution)/shard_map/ppermute | solution.py:19
  20.5 1.6 %collective-permute-start.27 = (bf16[128,512]{1,0:T(8,128)(2,1)S(1)}, bf16[128,512]{1,0:T(8,128)(2,1)S(1)}, u32[]{:S(2)}, u32[]{:S(2)}) collective-permute-start(bf16[128,512]{1,0:T(8,128)(2,1)S(1)} %collective-permute-done.26), channel_id=1, source_target_pairs={{0,1},{1,0},{2,3},{3,2},{4,5},{5,4},{6,7},{7,6},{8,9},{9,8},{10,11... | collective-permute-start | bytes 393224 | tf_op jit(solution)/shard_map/ppermute | solution.py:19
  20.7 8.3 %collective-permute-start.6 = (bf16[2,112,384]{2,1,0:T(8,128)(2,1)S(1)}, bf16[2,112,384]{2,1,0:T(8,128)(2,1)S(1)}, u32[]{:S(2)}, u32[]{:S(2)}) collective-permute-start(bf16[2,112,384]{2,1,0:T(8,128)(2,1)S(1)} %dynamic-slice_bitcast_fusion.5), channel_id=1, source_target_pairs={{0,4},{4,0},{8,12},{12,8},{16,20},{20,16},{24,28},{28,24},{1,5},{5... | collective-permute-start | bytes 516104 | tf_op jit(solution)/shard_map/ppermute | solution.py:19
  21.2 8.2 %collective-permute-start.14 = (bf16[2,112,384]{2,1,0:T(8,128)(2,1)S(1)}, bf16[2,112,384]{2,1,0:T(8,128)(2,1)S(1)}, u32[]{:S(2)}, u32[]{:S(2)}) collective-permute-start(bf16[2,112,384]{2,1,0:T(8,128)(2,1)S(1)} %dynamic-slice_bitcast_fusion.3), channel_id=1, source_target_pairs={{0,8},{4,12},{8,0},{12,4},{16,24},{20,28},{24,16},{28,20},{1,9},{5... | collective-permute-start | bytes 516104 | tf_op jit(solution)/shard_map/ppermute | solution.py:19
  23.2 17.9 %collective-permute-start.28 = (bf16[2,112,384]{2,1,0:T(8,128)(2,1)S(1)}, bf16[2,112,384]{2,1,0:T(8,128)(2,1)S(1)}, u32[]{:S(2)}, u32[]{:S(2)}) collective-permute-start(bf16[2,112,384]{2,1,0:T(8,128)(2,1)S(1)} %dynamic-slice_bitcast_fusion.1), channel_id=1, source_target_pairs={{0,4},{4,0},{8,12},{12,8},{16,20},{20,16},{24,28},{28,24},{1,5},{5... | collective-permute-start | bytes 516104 | tf_op jit(solution)/shard_map/ppermute | solution.py:19
  24.5 17.0 %collective-permute-start.33 = (bf16[2,112,384]{2,1,0:T(8,128)(2,1)S(1)}, bf16[2,112,384]{2,1,0:T(8,128)(2,1)S(1)}, u32[]{:S(2)}, u32[]{:S(2)}) collective-permute-start(bf16[2,112,384]{2,1,0:T(8,128)(2,1)S(1)} %dynamic-slice_bitcast_fusion), channel_id=1, source_target_pairs={{0,8},{4,12},{8,0},{12,4},{16,24},{20,28},{24,16},{28,20},{1,9},{5... | collective-permute-start | bytes 516104 | tf_op jit(solution)/shard_map/ppermute | solution.py:19
  26.2 7.5 %collective-permute-start.10 = (bf16[112,384]{1,0:T(8,128)(2,1)S(1)}, bf16[112,384]{1,0:T(8,128)(2,1)S(1)}, u32[]{:S(2)}, u32[]{:S(2)}) collective-permute-start(bf16[112,384]{1,0:T(8,128)(2,1)S(1)} %fusion.35), channel_id=1, source_target_pairs={{0,4},{4,0},{8,12},{12,8},{16,20},{20,16},{24,28},{28,24},{1,5},{5... | collective-permute-start | bytes 258056 | tf_op jit(solution)/shard_map/ppermute | solution.py:19
  28.9 6.4 %collective-permute-start.18 = (bf16[112,384]{1,0:T(8,128)(2,1)S(1)}, bf16[112,384]{1,0:T(8,128)(2,1)S(1)}, u32[]{:S(2)}, u32[]{:S(2)}) collective-permute-start(bf16[112,384]{1,0:T(8,128)(2,1)S(1)} %fusion.37), channel_id=1, source_target_pairs={{0,8},{4,12},{8,0},{12,4},{16,24},{20,28},{24,16},{28,20},{1,9},{5... | collective-permute-start | bytes 258056 | tf_op jit(solution)/shard_map/ppermute | solution.py:19
  29.4 8.5 %collective-permute-start.7 = (bf16[112,384]{1,0:T(8,128)(2,1)S(1)}, bf16[112,384]{1,0:T(8,128)(2,1)S(1)}, u32[]{:S(2)}, u32[]{:S(2)}) collective-permute-start(bf16[112,384]{1,0:T(8,128)(2,1)S(1)} %fusion.34), channel_id=1, source_target_pairs={{0,8},{4,12},{8,0},{12,4},{16,24},{20,28},{24,16},{28,20},{1,9},{5... | collective-permute-start | bytes 258056 | tf_op jit(solution)/shard_map/ppermute | solution.py:19
  33.7 4.7 %collective-permute-start.15 = (bf16[112,384]{1,0:T(8,128)(2,1)S(1)}, bf16[112,384]{1,0:T(8,128)(2,1)S(1)}, u32[]{:S(2)}, u32[]{:S(2)}) collective-permute-start(bf16[112,384]{1,0:T(8,128)(2,1)S(1)} %fusion.36), channel_id=1, source_target_pairs={{0,4},{4,0},{8,12},{12,8},{16,20},{20,16},{24,28},{28,24},{1,5},{5... | collective-permute-start | bytes 258056 | tf_op jit(solution)/shard_map/ppermute | solution.py:19
  35.3 17.9 %collective-permute-start.11 = (bf16[112,384]{1,0:T(8,128)(2,1)S(1)}, bf16[112,384]{1,0:T(8,128)(2,1)S(1)}, u32[]{:S(2)}, u32[]{:S(2)}) collective-permute-start(bf16[112,384]{1,0:T(8,128)(2,1)S(1)} %fusion.22), channel_id=1, source_target_pairs={{0,16},{4,20},{8,24},{12,28},{16,0},{20,4},{24,8},{28,12},{1,17},{... | collective-permute-start | bytes 258056 | tf_op jit(solution)/shard_map/ppermute | solution.py:19
  38.0 21.5 %collective-permute-start.19 = (bf16[112,384]{1,0:T(8,128)(2,1)S(1)}, bf16[112,384]{1,0:T(8,128)(2,1)S(1)}, u32[]{:S(2)}, u32[]{:S(2)}) collective-permute-start(bf16[112,384]{1,0:T(8,128)(2,1)S(1)} %fusion.20), channel_id=1, source_target_pairs={{0,16},{4,20},{8,24},{12,28},{16,0},{20,4},{24,8},{28,12},{1,17},{... | collective-permute-start | bytes 258056 | tf_op jit(solution)/shard_map/ppermute | solution.py:19
  38.4 15.8 %collective-permute-start.8 = (bf16[112,384]{1,0:T(8,128)(2,1)S(1)}, bf16[112,384]{1,0:T(8,128)(2,1)S(1)}, u32[]{:S(2)}, u32[]{:S(2)}) collective-permute-start(bf16[112,384]{1,0:T(8,128)(2,1)S(1)} %fusion.23), channel_id=1, source_target_pairs={{0,16},{4,20},{8,24},{12,28},{16,0},{20,4},{24,8},{28,12},{1,17},{... | collective-permute-start | bytes 258056 | tf_op jit(solution)/shard_map/ppermute | solution.py:19
  41.1 19.0 %collective-permute-start.16 = (bf16[112,384]{1,0:T(8,128)(2,1)S(1)}, bf16[112,384]{1,0:T(8,128)(2,1)S(1)}, u32[]{:S(2)}, u32[]{:S(2)}) collective-permute-start(bf16[112,384]{1,0:T(8,128)(2,1)S(1)} %fusion.21), channel_id=1, source_target_pairs={{0,16},{4,20},{8,24},{12,28},{16,0},{20,4},{24,8},{28,12},{1,17},{... | collective-permute-start | bytes 258056 | tf_op jit(solution)/shard_map/ppermute | solution.py:19
  41.6 5.1 %collective-permute-start.29 = (bf16[112,384]{1,0:T(8,128)(2,1)S(1)}, bf16[112,384]{1,0:T(8,128)(2,1)S(1)}, u32[]{:S(2)}, u32[]{:S(2)}) collective-permute-start(bf16[112,384]{1,0:T(8,128)(2,1)S(1)} %fusion.38), channel_id=1, source_target_pairs={{0,8},{4,12},{8,0},{12,4},{16,24},{20,28},{24,16},{28,20},{1,9},{5... | collective-permute-start | bytes 258056 | tf_op jit(solution)/shard_map/ppermute | solution.py:19
  46.7 4.5 %collective-permute-start.34 = (bf16[112,384]{1,0:T(8,128)(2,1)S(1)}, bf16[112,384]{1,0:T(8,128)(2,1)S(1)}, u32[]{:S(2)}, u32[]{:S(2)}) collective-permute-start(bf16[112,384]{1,0:T(8,128)(2,1)S(1)} %fusion.39), channel_id=1, source_target_pairs={{0,4},{4,0},{8,12},{12,8},{16,20},{20,16},{24,28},{28,24},{1,5},{5... | collective-permute-start | bytes 258056 | tf_op jit(solution)/shard_map/ppermute | solution.py:19
  51.2 6.3 %collective-permute-start.30 = (bf16[112,384]{1,0:T(8,128)(2,1)S(1)}, bf16[112,384]{1,0:T(8,128)(2,1)S(1)}, u32[]{:S(2)}, u32[]{:S(2)}) collective-permute-start(bf16[112,384]{1,0:T(8,128)(2,1)S(1)} %fusion.19), channel_id=1, source_target_pairs={{0,16},{4,20},{8,24},{12,28},{16,0},{20,4},{24,8},{28,12},{1,17},{... | collective-permute-start | bytes 258056 | tf_op jit(solution)/shard_map/ppermute | solution.py:19
  53.2 6.9 %collective-permute-start.35 = (bf16[112,384]{1,0:T(8,128)(2,1)S(1)}, bf16[112,384]{1,0:T(8,128)(2,1)S(1)}, u32[]{:S(2)}, u32[]{:S(2)}) collective-permute-start(bf16[112,384]{1,0:T(8,128)(2,1)S(1)} %fusion.18), channel_id=1, source_target_pairs={{0,16},{4,20},{8,24},{12,28},{16,0},{20,4},{24,8},{28,12},{1,17},{... | collective-permute-start | bytes 258056 | tf_op jit(solution)/shard_map/ppermute | solution.py:19
  57.6 5.8 %collective-permute-start.38 = (bf16[112,384]{1,0:T(8,128)(2,1)S(1)}, bf16[112,384]{1,0:T(8,128)(2,1)S(1)}, u32[]{:S(2)}, u32[]{:S(2)}) collective-permute-start(bf16[112,384]{1,0:T(8,128)(2,1)S(1)} %get-tuple-element.27), channel_id=1, source_target_pairs={{0,8},{4,12},{8,0},{12,4},{16,24},{20,28},{24,16},{28,20},{1,9},{5... | collective-permute-start | bytes 258056 | tf_op jit(solution)/shard_map/ppermute | solution.py:19
  59.1 5.4 %collective-permute-start.31 = (bf16[112,384]{1,0:T(8,128)(2,1)S(1)}, bf16[112,384]{1,0:T(8,128)(2,1)S(1)}, u32[]{:S(2)}, u32[]{:S(2)}) collective-permute-start(bf16[112,384]{1,0:T(8,128)(2,1)S(1)} %get-tuple-element.28), channel_id=1, source_target_pairs={{0,4},{4,0},{8,12},{12,8},{16,20},{20,16},{24,28},{28,24},{1,5},{5... | collective-permute-start | bytes 258056 | tf_op jit(solution)/shard_map/ppermute | solution.py:19
  59.5 6.0 %collective-permute-start.12 = (bf16[112,384]{1,0:T(8,128)(2,1)S(1)}, bf16[112,384]{1,0:T(8,128)(2,1)S(1)}, u32[]{:S(2)}, u32[]{:S(2)}) collective-permute-start(bf16[112,384]{1,0:T(8,128)(2,1)S(1)} %get-tuple-element.29), channel_id=1, source_target_pairs={{0,8},{4,12},{8,0},{12,4},{16,24},{20,28},{24,16},{28,20},{1,9},{5... | collective-permute-start | bytes 258056 | tf_op jit(solution)/shard_map/ppermute | solution.py:19
  60.3 6.0 %collective-permute-start.40 = (bf16[112,384]{1,0:T(8,128)(2,1)S(1)}, bf16[112,384]{1,0:T(8,128)(2,1)S(1)}, u32[]{:S(2)}, u32[]{:S(2)}) collective-permute-start(bf16[112,384]{1,0:T(8,128)(2,1)S(1)} %get-tuple-element.30), channel_id=1, source_target_pairs={{0,4},{4,0},{8,12},{12,8},{16,20},{20,16},{24,28},{28,24},{1,5},{5... | collective-permute-start | bytes 258056 | tf_op jit(solution)/shard_map/ppermute | solution.py:19
  61.9 7.5 %collective-permute-start.36 = (bf16[112,384]{1,0:T(8,128)(2,1)S(1)}, bf16[112,384]{1,0:T(8,128)(2,1)S(1)}, u32[]{:S(2)}, u32[]{:S(2)}) collective-permute-start(bf16[112,384]{1,0:T(8,128)(2,1)S(1)} %get-tuple-element.31), channel_id=1, source_target_pairs={{0,8},{4,12},{8,0},{12,4},{16,24},{20,28},{24,16},{28,20},{1,9},{5... | collective-permute-start | bytes 258056 | tf_op jit(solution)/shard_map/ppermute | solution.py:19
  63.3 5.0 %collective-permute-start.20 = (bf16[112,384]{1,0:T(8,128)(2,1)S(1)}, bf16[112,384]{1,0:T(8,128)(2,1)S(1)}, u32[]{:S(2)}, u32[]{:S(2)}) collective-permute-start(bf16[112,384]{1,0:T(8,128)(2,1)S(1)} %get-tuple-element.32), channel_id=1, source_target_pairs={{0,4},{4,0},{8,12},{12,8},{16,20},{20,16},{24,28},{28,24},{1,5},{5... | collective-permute-start | bytes 258056 | tf_op jit(solution)/shard_map/ppermute | solution.py:19
  64.5 18.6 %collective-permute-start.39 = (bf16[2,112,384]{2,1,0:T(8,128)(2,1)S(1)}, bf16[2,112,384]{2,1,0:T(8,128)(2,1)S(1)}, u32[]{:S(2)}, u32[]{:S(2)}) collective-permute-start(bf16[2,112,384]{2,1,0:T(8,128)(2,1)S(1)} %maximum_select_fusion.14), channel_id=1, source_target_pairs={{0,4},{4,0},{8,12},{12,8},{16,20},{20,16},{24,28},{28,24},{1,5},{5... | collective-permute-start | bytes 516104 | tf_op jit(solution)/shard_map/ppermute | solution.py:19
  65.5 10.8 %collective-permute-start.32 = (bf16[2,112,384]{2,1,0:T(8,128)(2,1)S(1)}, bf16[2,112,384]{2,1,0:T(8,128)(2,1)S(1)}, u32[]{:S(2)}, u32[]{:S(2)}) collective-permute-start(bf16[2,112,384]{2,1,0:T(8,128)(2,1)S(1)} %maximum_select_fusion.10), channel_id=1, source_target_pairs={{0,8},{4,12},{8,0},{12,4},{16,24},{20,28},{24,16},{28,20},{1,9},{5... | collective-permute-start | bytes 516104 | tf_op jit(solution)/shard_map/ppermute | solution.py:19
  66.3 7.1 %collective-permute-start.13 = (bf16[2,112,384]{2,1,0:T(8,128)(2,1)S(1)}, bf16[2,112,384]{2,1,0:T(8,128)(2,1)S(1)}, u32[]{:S(2)}, u32[]{:S(2)}) collective-permute-start(bf16[2,112,384]{2,1,0:T(8,128)(2,1)S(1)} %maximum_select_fusion.6), channel_id=1, source_target_pairs={{0,4},{4,0},{8,12},{12,8},{16,20},{20,16},{24,28},{28,24},{1,5},{5... | collective-permute-start | bytes 516104 | tf_op jit(solution)/shard_map/ppermute | solution.py:19
  68.4 14.5 %collective-permute-start.41 = (bf16[2,112,384]{2,1,0:T(8,128)(2,1)S(1)}, bf16[2,112,384]{2,1,0:T(8,128)(2,1)S(1)}, u32[]{:S(2)}, u32[]{:S(2)}) collective-permute-start(bf16[2,112,384]{2,1,0:T(8,128)(2,1)S(1)} %maximum_select_fusion.16), channel_id=1, source_target_pairs={{0,8},{4,12},{8,0},{12,4},{16,24},{20,28},{24,16},{28,20},{1,9},{5... | collective-permute-start | bytes 516104 | tf_op jit(solution)/shard_map/ppermute | solution.py:19
  69.4 6.2 %collective-permute-start.21 = (bf16[2,112,384]{2,1,0:T(8,128)(2,1)S(1)}, bf16[2,112,384]{2,1,0:T(8,128)(2,1)S(1)}, u32[]{:S(2)}, u32[]{:S(2)}) collective-permute-start(bf16[2,112,384]{2,1,0:T(8,128)(2,1)S(1)} %maximum_select_fusion.8), channel_id=1, source_target_pairs={{0,8},{4,12},{8,0},{12,4},{16,24},{20,28},{24,16},{28,20},{1,9},{5... | collective-permute-start | bytes 516104 | tf_op jit(solution)/shard_map/ppermute | solution.py:19
  73.4 5.4 %collective-permute-start.37 = (bf16[2,112,384]{2,1,0:T(8,128)(2,1)S(1)}, bf16[2,112,384]{2,1,0:T(8,128)(2,1)S(1)}, u32[]{:S(2)}, u32[]{:S(2)}) collective-permute-start(bf16[2,112,384]{2,1,0:T(8,128)(2,1)S(1)} %maximum_select_fusion.12), channel_id=1, source_target_pairs={{0,4},{4,0},{8,12},{12,8},{16,20},{20,16},{24,28},{28,24},{1,5},{5... | collective-permute-start | bytes 516104 | tf_op jit(solution)/shard_map/ppermute | solution.py:19
  76.3 11.8 %collective-permute-start.22 = (bf16[2,56,512]{2,1,0:T(8,128)(2,1)S(1)}, bf16[2,56,512]{2,1,0:T(8,128)(2,1)S(1)}, u32[]{:S(2)}, u32[]{:S(2)}) collective-permute-start(bf16[2,56,512]{2,1,0:T(8,128)(2,1)S(1)} %get-tuple-element.24), channel_id=1, source_target_pairs={{0,1},{1,0},{2,3},{3,2},{4,5},{5,4},{6,7},{7,6},{8,9},{9,8},{10,11... | collective-permute-start | bytes 344072 | tf_op jit(solution)/shard_map/ppermute | solution.py:19
  76.3 13.3 %collective-permute-start.24 = (bf16[2,56,512]{2,1,0:T(8,128)(2,1)S(1)}, bf16[2,56,512]{2,1,0:T(8,128)(2,1)S(1)}, u32[]{:S(2)}, u32[]{:S(2)}) collective-permute-start(bf16[2,56,512]{2,1,0:T(8,128)(2,1)S(1)} %get-tuple-element.25), channel_id=1, source_target_pairs={{0,3},{1,2},{2,1},{3,0},{4,7},{5,6},{6,5},{7,4},{8,11},{9,10},{10,... | collective-permute-start | bytes 344072 | tf_op jit(solution)/shard_map/ppermute | solution.py:19
  78.8 10.8 %collective-permute-start.23 = (bf16[2,56,512]{2,1,0:T(8,128)(2,1)S(1)}, bf16[2,56,512]{2,1,0:T(8,128)(2,1)S(1)}, u32[]{:S(2)}, u32[]{:S(2)}) collective-permute-start(bf16[2,56,512]{2,1,0:T(8,128)(2,1)S(1)} %get-tuple-element.26), channel_id=1, source_target_pairs={{0,2},{1,3},{2,0},{3,1},{4,6},{5,7},{6,4},{7,5},{8,10},{9,11},{10,... | collective-permute-start | bytes 344072 | tf_op jit(solution)/shard_map/ppermute | solution.py:19
  83.9 6.9 %collective-permute-start.42 = (bf16[2,56,512]{2,1,0:T(8,128)(2,1)S(1)}, bf16[2,56,512]{2,1,0:T(8,128)(2,1)S(1)}, u32[]{:S(2)}, u32[]{:S(2)}) collective-permute-start(bf16[2,56,512]{2,1,0:T(8,128)(2,1)S(1)} %get-tuple-element.20), channel_id=1, source_target_pairs={{0,1},{1,0},{2,3},{3,2},{4,5},{5,4},{6,7},{7,6},{8,9},{9,8},{10,11... | collective-permute-start | bytes 344072 | tf_op jit(solution)/shard_map/ppermute | solution.py:19
  84.0 6.8 %collective-permute-start.44 = (bf16[2,56,512]{2,1,0:T(8,128)(2,1)S(1)}, bf16[2,56,512]{2,1,0:T(8,128)(2,1)S(1)}, u32[]{:S(2)}, u32[]{:S(2)}) collective-permute-start(bf16[2,56,512]{2,1,0:T(8,128)(2,1)S(1)} %get-tuple-element.21), channel_id=1, source_target_pairs={{0,3},{1,2},{2,1},{3,0},{4,7},{5,6},{6,5},{7,4},{8,11},{9,10},{10,... | collective-permute-start | bytes 344072 | tf_op jit(solution)/shard_map/ppermute | solution.py:19
  86.3 3.4 %copy-start.3 = (f32[128,2]{0,1:T(2,128)S(1)}, f32[128,2]{0,1:T(2,128)}, u32[]{:S(2)}) copy-start(f32[128,2]{0,1:T(2,128)} %param.10) | copy-start | bytes 3076
  88.0 5.1 %collective-permute-start.43 = (bf16[2,56,512]{2,1,0:T(8,128)(2,1)S(1)}, bf16[2,56,512]{2,1,0:T(8,128)(2,1)S(1)}, u32[]{:S(2)}, u32[]{:S(2)}) collective-permute-start(bf16[2,56,512]{2,1,0:T(8,128)(2,1)S(1)} %get-tuple-element.22), channel_id=1, source_target_pairs={{0,2},{1,3},{2,0},{3,1},{4,6},{5,7},{6,4},{7,5},{8,10},{9,11},{10,... | collective-permute-start | bytes 344072 | tf_op jit(solution)/shard_map/ppermute | solution.py:19
  (1 other events, 3.4 us)
where the time goes:
time: 94.4 us; the launch traced here: 94.1 us
  starting transfers between devices  44.9 us (48%)
  waiting for transfers between devices  27.3 us (29%)
  matrix products  14.2 us (15%)
  other arithmetic  5.67 us (6%)
  between operations  1.35 us (1%)
    ppermute x45, starting transfers between devices, swap(): return lax.ppermute(x, axis, [(i, i ^ k) for i in range(n)])  44.9 us
    ppermute x45, waiting for transfers between devices, swap(): return lax.ppermute(x, axis, [(i, i ^ k) for i in range(n)])  27.3 us
    dot_general x21, matrix products, mm(): return jnp.einsum(form, a, b, preferred_element_type=F32)  14.2 us
  transfers between devices with their start and end apart: 45, of which 14 were waited for; matrix products, arithmetic and copies ran while one was open for 19% of the time, Pallas kernels for 0%

commit v1 on v0

--- a/solution.py
+++ b/solution.py
@@ -67,7 +67,7 @@
     return (lax.axis_index("dp") // k) % 2
 
 
-def sum_rows(x, crossed=False):
+def sum_rows(x, crossed):
     n = lax.axis_size("dp")
     if not power_of_two(n):
         return lax.psum_scatter(x, "dp", scatter_dimension=0, tiled=True).astype(F32)
@@ -84,11 +84,12 @@
         x = mine.astype(F32) + got.astype(F32)
     if n > 1:
         x = x.astype(BF)
-        x = x.astype(F32) + swap(x, "dp", n // 2).astype(F32)
+        got = swap(x, "dp", n // 2)
+        x = x.astype(F32) + got.astype(F32)
     return x
 
 
-def gather_rows(x, crossed=False):
+def gather_rows(x, crossed):
     n = lax.axis_size("dp")
     if not power_of_two(n):
         return lax.all_gather(x, "dp", axis=0, tiled=True)
@@ -119,28 +120,35 @@
 
     meta = jnp.concatenate((expert_ids.T.astype(F32), probs.T), axis=0)
     token_blocks = gather_peers(tokens)
-    metas = jnp.stack(gather_peers(meta))
+    metas = gather_peers(meta)
     cot_blocks = gather_peers(cotangent, token_blocks[shards // 2])
 
     earlier = (
         jnp.arange(token_count)[:, None] < jnp.arange(token_count)[None, :]
     ).astype(BF)
 
-    ids_in = metas[:, :top, :].astype(jnp.int32)
-    probs_in = metas[:, top:, :]
-    mine = (me * held + jnp.arange(held))[:, None, None, None]
-    named = ids_in[None] == mine
-    hit = jnp.any(named, axis=2)
-    weight_of = jnp.sum(jnp.where(named, probs_in[None], 0.0), axis=2)
-    place = mm("jst,tu->jsu", hit.astype(BF), earlier).astype(jnp.int32)
-    slots = jnp.arange(capacity)[None, None, :, None]
-    chosen = hit[:, :, None, :] & (place[:, :, None, :] == slots)
-    pick = chosen.astype(BF)
-    slot_prob = jnp.sum(jnp.where(chosen, weight_of[:, :, None, :], 0.0), axis=3)
+    def picks(metas):
+        ids_in = metas[:, :top, :].astype(jnp.int32)
+        probs_in = metas[:, top:, :]
+        mine = (me * held + jnp.arange(held))[:, None, None, None]
+        named = ids_in[None] == mine
+        hit = jnp.any(named, axis=2)
+        weight_of = jnp.sum(jnp.where(named, probs_in[None], 0.0), axis=2)
+        place = mm("jst,tu->jsu", hit.astype(BF), earlier).astype(jnp.int32)
+        slots = jnp.arange(capacity)[None, None, :, None]
+        chosen = hit[:, :, None, :] & (place[:, :, None, :] == slots)
+        slot_prob = jnp.sum(jnp.where(chosen, weight_of[:, :, None, :], 0.0), axis=3)
+        return chosen.astype(BF), slot_prob
+
+    pick, slot_prob = picks(jnp.stack(metas))
 
     rows_in = jnp.stack(
         [mm("jct,td->jcd", pick[:, k], token_blocks[k]).astype(BF) for k in range(shards)], axis=1
     )
+    rows_in = rows_in.reshape(held, rows, slice_width)
+    gate_part = mm("jrd,jdf->jrf", rows_in, gate_weight).astype(BF).reshape(held * rows, units)
+    up_part = mm("jrd,jdf->jrf", rows_in, up_weight).astype(BF).reshape(held * rows, units)
+    up_part, pick = lax.optimization_barrier((up_part, pick))
     grad_out = jnp.stack(
         [
             (slot_prob[:, k, :, None] * mm("jct,td->jcd", pick[:, k], cot_blocks[k])).astype(BF)
@@ -148,9 +156,6 @@
         ],
         axis=1,
     ).reshape(held, rows, slice_width)
-    rows_in = rows_in.reshape(held, rows, slice_width)
-    gate_part = mm("jrd,jdf->jrf", rows_in, gate_weight).astype(BF).reshape(held * rows, units)
-    up_part = mm("jrd,jdf->jrf", rows_in, up_weight).astype(BF).reshape(held * rows, units)
     grad_part = mm("jrd,jfd->jrf", grad_out, down_weight).astype(BF).reshape(held * rows, units)
 
     cuts = CUTS if units % (128 * CUTS) == 0 else 1
@@ -177,14 +182,13 @@
     expert_out = mm("jrf,jfd->jrd", hidden, down_weight).astype(BF)
     expert_out = expert_out.reshape(held, shards, capacity, slice_width)
     returned = exchange_peers([expert_out[:, k] for k in range(shards)])
-    grad_down = mm("jrf,jrd->jfd", hidden, grad_out).astype(BF)
-
     grad_row = (
         mm("jrf,jdf->jrd", gg, gate_weight) + mm("jrf,jdf->jrd", gu, up_weight)
     ).astype(BF)
-    gg, gu, grad_row = lax.optimization_barrier((gg, gu, grad_row))
+    hidden, gg, gu, grad_row = lax.optimization_barrier((hidden, gg, gu, grad_row))
     grad_row = grad_row.reshape(held, shards, capacity, slice_width)
     grad_back = exchange_peers([grad_row[:, k] for k in range(shards)])
+    grad_down = mm("jrf,jrd->jfd", hidden, grad_out).astype(BF)
     grad_gate = mm("jrd,jrf->jdf", rows_in, gg).astype(BF)
     grad_up = mm("jrd,jrf->jdf", rows_in, gu).astype(BF)
 
@@ -199,7 +203,8 @@
     grad_rows = jnp.concatenate(grad_back).reshape(experts * capacity, slice_width)
     out_pairs = mm("ktr,rd->ktd", back, out_rows)
     mixed = jnp.sum(probs.T[:, :, None] * out_pairs, axis=0).astype(BF)
-    grad_tokens = mm("tr,rd->td", jnp.sum(back, axis=0), grad_rows).astype(BF)
+    either = lax.optimization_barrier(jnp.sum(back, axis=0))
+    grad_tokens = mm("tr,rd->td", either, grad_rows).astype(BF)
     return (mixed, grad_tokens, grad_gate, grad_up, grad_down)
 
 

time: 94.4 us -> 97.3 us (1.031)
  starting transfers between devices: 44.9 us -> 49.4 us
  matrix products: 14.2 us -> 13.2 us
    ppermute x45, starting transfers between devices: 44.9 us -> 49.4 us  [swap(): return lax.ppermute(x, axis, [(i, i ^ k) for i in range(n)])]
    dot_general x21, matrix products: 14.2 us -> 13.2 us  [mm(): return jnp.einsum(form, a, b, preferred_element_type=F32)]
  transfers between devices with their start and end apart: 45 -> 45, of which waited for: 14 -> 14; matrix products, arithmetic and copies ran while one was open for 19% -> 18% of each run, Pallas kernels for 0% -> 0%
where the time goes in v1:
time: 97.3 us; the launch traced here: 97.1 us
  starting transfers between devices  49.4 us (51%)
  waiting for transfers between devices  26.4 us (27%)
  matrix products  13.2 us (14%)
  other arithmetic  5.73 us (6%)
  between operations  1.4 us (1%)
    ppermute x45, starting transfers between devices, swap(): return lax.ppermute(x, axis, [(i, i ^ k) for i in range(n)])  49.4 us
    ppermute x45, waiting for transfers between devices, swap(): return lax.ppermute(x, axis, [(i, i ^ k) for i in range(n)])  26.4 us
    dot_general x21, matrix products, mm(): return jnp.einsum(form, a, b, preferred_element_type=F32)  13.2 us
  transfers between devices with their start and end apart: 45, of which 14 were waited for; matrix products, arithmetic and copies ran while one was open for 18% of the time, Pallas kernels for 0%

profile of v1, /device:TPU:0, one launch (start us, length us, event | category | flops | bytes accessed | tf_op | source)
XLA Modules:
  0.0 97.1 jit_solution(15893359911129696172)
XLA Ops:
  0.6 0.8 bitcast_convert_fusion
  1.4 0.7 pad_maximum_fusion.8
  2.1 3.0 %collective-permute-start.1 = (f32[4,128]{1,0:T(4,128)S(1)}, f32[4,128]{1,0:T(4,128)S(1)}, u32[]{:S(2)}, u32[]{:S(2)}) collective-permute-start(f32[4,128]{1,0:T(4,128)S(1)} %pad_maximum_fusion.8), channel_id=1, source_target_pairs={{0,2},{1,3},{2,0},{3,1},{4,6},{5,7},{6,4},{7,5},{8,10},{9,11},{10,... | collective-permute-start | bytes 6152 | tf_op jit(solution)/shard_map/ppermute | solution.py:19
  5.8 0.7 fusion.51
  6.6 0.7 select_reduce_fusion.1
  7.3 0.7 multiply_add_fusion
  8.5 0.8 collective-permute-done.2
  9.9 1.1 %fusion.6 = bf16[2,1,56,512]{3,2,0,1:T(8,128)(2,1)S(1)} fusion(bf16[128,512]{1,0:T(8,128)(2,1)} %param.7, pred[2,4,56,128]{3,2,0,1:T(8,128)(4,1)S(1)} %get-tuple-element.42), kind=kOutput, calls=%fused_computation.24 | convolution fusion | flops 14737408 | bytes 260096 | tf_op jit(solution)/shard_map/jct,td->jcd/dot_general | solution.py:107
  11.2 1.7 %collective-permute-start.26 = (bf16[128,512]{1,0:T(8,128)(2,1)}, bf16[128,512]{1,0:T(8,128)(2,1)S(1)}, u32[]{:S(2)}, u32[]{:S(2)}) collective-permute-start(bf16[128,512]{1,0:T(8,128)(2,1)} %param.8), channel_id=1, source_target_pairs={{0,2},{1,3},{2,0},{3,1},{4,6},{5,7},{6,4},{7,5},{8,10},{9,11},{10,... | collective-permute-start | bytes 393224 | tf_op jit(solution)/shard_map/ppermute | solution.py:19
  13.3 1.0 %collective-permute-done.5 = bf16[128,512]{1,0:T(8,128)(2,1)S(1)} collective-permute-done((bf16[128,512]{1,0:T(8,128)(2,1)S(1)}, bf16[128,512]{1,0:T(8,128)(2,1)S(1)}, u32[]{:S(2)}, u32[]{:S(2)}) %collective-permute-start.5) | collective-permute-done | bytes 131104 | tf_op jit(solution)/shard_map/ppermute | solution.py:19
  15.2 1.6 %collective-permute-start.9 = (bf16[2,112,384]{2,1,0:T(8,128)(2,1)S(1)}, bf16[2,112,384]{2,1,0:T(8,128)(2,1)S(1)}, u32[]{:S(2)}, u32[]{:S(2)}) collective-permute-start(bf16[2,112,384]{2,1,0:T(8,128)(2,1)S(1)} %dynamic-slice_bitcast_fusion.4), channel_id=1, source_target_pairs={{0,8},{4,12},{8,0},{12,4},{16,24},{20,28},{24,16},{28,20},{1,9},{5... | collective-permute-start | bytes 516104 | tf_op jit(solution)/shard_map/ppermute | solution.py:19
  16.9 1.6 %collective-permute-start.17 = (bf16[2,112,384]{2,1,0:T(8,128)(2,1)S(1)}, bf16[2,112,384]{2,1,0:T(8,128)(2,1)S(1)}, u32[]{:S(2)}, u32[]{:S(2)}) collective-permute-start(bf16[2,112,384]{2,1,0:T(8,128)(2,1)S(1)} %dynamic-slice_bitcast_fusion.2), channel_id=1, source_target_pairs={{0,4},{4,0},{8,12},{12,8},{16,20},{20,16},{24,28},{28,24},{1,5},{5... | collective-permute-start | bytes 516104 | tf_op jit(solution)/shard_map/ppermute | solution.py:19
  21.8 0.6 convolution_convert_fusion.3
  22.6 1.4 %collective-permute-start.28 = (bf16[2,112,384]{2,1,0:T(8,128)(2,1)S(1)}, bf16[2,112,384]{2,1,0:T(8,128)(2,1)S(1)}, u32[]{:S(2)}, u32[]{:S(2)}) collective-permute-start(bf16[2,112,384]{2,1,0:T(8,128)(2,1)S(1)} %dynamic-slice_bitcast_fusion.1), channel_id=1, source_target_pairs={{0,4},{4,0},{8,12},{12,8},{16,20},{20,16},{24,28},{28,24},{1,5},{5... | collective-permute-start | bytes 516104 | tf_op jit(solution)/shard_map/ppermute | solution.py:19
  24.0 1.2 %collective-permute-start.33 = (bf16[2,112,384]{2,1,0:T(8,128)(2,1)S(1)}, bf16[2,112,384]{2,1,0:T(8,128)(2,1)S(1)}, u32[]{:S(2)}, u32[]{:S(2)}) collective-permute-start(bf16[2,112,384]{2,1,0:T(8,128)(2,1)S(1)} %dynamic-slice_bitcast_fusion), channel_id=1, source_target_pairs={{0,8},{4,12},{8,0},{12,4},{16,24},{20,28},{24,16},{28,20},{1,9},{5... | collective-permute-start | bytes 516104 | tf_op jit(solution)/shard_map/ppermute | solution.py:19
  25.3 0.7 collective-permute-start.10
  26.1 1.8 %collective-permute-done.6 = bf16[2,112,384]{2,1,0:T(8,128)(2,1)S(1)} collective-permute-done((bf16[2,112,384]{2,1,0:T(8,128)(2,1)S(1)}, bf16[2,112,384]{2,1,0:T(8,128)(2,1)S(1)}, u32[]{:S(2)}, u32[]{:S(2)}) %collective-permute-start.6) | collective-permute-done | bytes 172064 | tf_op jit(solution)/shard_map/ppermute | solution.py:19
  28.0 2.1 %collective-permute-start.7 = (bf16[112,384]{1,0:T(8,128)(2,1)S(1)}, bf16[112,384]{1,0:T(8,128)(2,1)S(1)}, u32[]{:S(2)}, u32[]{:S(2)}) collective-permute-start(bf16[112,384]{1,0:T(8,128)(2,1)S(1)} %fusion.34), channel_id=1, source_target_pairs={{0,8},{4,12},{8,0},{12,4},{16,24},{20,28},{24,16},{28,20},{1,9},{5... | collective-permute-start | bytes 258056 | tf_op jit(solution)/shard_map/ppermute | solution.py:19
  30.1 2.2 %collective-permute-done.10 = bf16[112,384]{1,0:T(8,128)(2,1)S(1)} collective-permute-done((bf16[112,384]{1,0:T(8,128)(2,1)S(1)}, bf16[112,384]{1,0:T(8,128)(2,1)S(1)}, u32[]{:S(2)}, u32[]{:S(2)}) %collective-permute-start.10) | collective-permute-done | bytes 86048 | tf_op jit(solution)/shard_map/ppermute | solution.py:19
  32.3 1.5 %collective-permute-start.15 = (bf16[112,384]{1,0:T(8,128)(2,1)S(1)}, bf16[112,384]{1,0:T(8,128)(2,1)S(1)}, u32[]{:S(2)}, u32[]{:S(2)}) collective-permute-start(bf16[112,384]{1,0:T(8,128)(2,1)S(1)} %fusion.36), channel_id=1, source_target_pairs={{0,4},{4,0},{8,12},{12,8},{16,20},{20,16},{24,28},{28,24},{1,5},{5... | collective-permute-start | bytes 258056 | tf_op jit(solution)/shard_map/ppermute | solution.py:19
  33.9 2.7 %collective-permute-start.11 = (bf16[112,384]{1,0:T(8,128)(2,1)S(1)}, bf16[112,384]{1,0:T(8,128)(2,1)S(1)}, u32[]{:S(2)}, u32[]{:S(2)}) collective-permute-start(bf16[112,384]{1,0:T(8,128)(2,1)S(1)} %fusion.22), channel_id=1, source_target_pairs={{0,16},{4,20},{8,24},{12,28},{16,0},{20,4},{24,8},{28,12},{1,17},{... | collective-permute-start | bytes 258056 | tf_op jit(solution)/shard_map/ppermute | solution.py:19
  36.6 0.9 collective-permute-start.19
  37.5 2.2 %collective-permute-start.8 = (bf16[112,384]{1,0:T(8,128)(2,1)S(1)}, bf16[112,384]{1,0:T(8,128)(2,1)S(1)}, u32[]{:S(2)}, u32[]{:S(2)}) collective-permute-start(bf16[112,384]{1,0:T(8,128)(2,1)S(1)} %fusion.23), channel_id=1, source_target_pairs={{0,16},{4,20},{8,24},{12,28},{16,0},{20,4},{24,8},{28,12},{1,17},{... | collective-permute-start | bytes 258056 | tf_op jit(solution)/shard_map/ppermute | solution.py:19
  39.7 0.9 collective-permute-start.16
  41.0 4.5 %collective-permute-done.29 = bf16[112,384]{1,0:T(8,128)(2,1)S(1)} collective-permute-done((bf16[112,384]{1,0:T(8,128)(2,1)S(1)}, bf16[112,384]{1,0:T(8,128)(2,1)S(1)}, u32[]{:S(2)}, u32[]{:S(2)}) %collective-permute-start.29) | collective-permute-done | bytes 86048 | tf_op jit(solution)/shard_map/ppermute | solution.py:19
  45.5 6.6 %collective-permute-start.34 = (bf16[112,384]{1,0:T(8,128)(2,1)S(1)}, bf16[112,384]{1,0:T(8,128)(2,1)S(1)}, u32[]{:S(2)}, u32[]{:S(2)}) collective-permute-start(bf16[112,384]{1,0:T(8,128)(2,1)S(1)} %fusion.39), channel_id=1, source_target_pairs={{0,4},{4,0},{8,12},{12,8},{16,20},{20,16},{24,28},{28,24},{1,5},{5... | collective-permute-start | bytes 258056 | tf_op jit(solution)/shard_map/ppermute | solution.py:19
  52.2 2.4 %collective-permute-done.34 = bf16[112,384]{1,0:T(8,128)(2,1)S(1)} collective-permute-done((bf16[112,384]{1,0:T(8,128)(2,1)S(1)}, bf16[112,384]{1,0:T(8,128)(2,1)S(1)}, u32[]{:S(2)}, u32[]{:S(2)}) %collective-permute-start.34) | collective-permute-done | bytes 86048 | tf_op jit(solution)/shard_map/ppermute | solution.py:19
  54.7 3.0 %collective-permute-start.35 = (bf16[112,384]{1,0:T(8,128)(2,1)S(1)}, bf16[112,384]{1,0:T(8,128)(2,1)S(1)}, u32[]{:S(2)}, u32[]{:S(2)}) collective-permute-start(bf16[112,384]{1,0:T(8,128)(2,1)S(1)} %fusion.18), channel_id=1, source_target_pairs={{0,16},{4,20},{8,24},{12,28},{16,0},{20,4},{24,8},{28,12},{1,17},{... | collective-permute-start | bytes 258056 | tf_op jit(solution)/shard_map/ppermute | solution.py:19
  57.7 3.4 %collective-permute-done.30 = bf16[112,384]{1,0:T(8,128)(2,1)S(1)} collective-permute-done((bf16[112,384]{1,0:T(8,128)(2,1)S(1)}, bf16[112,384]{1,0:T(8,128)(2,1)S(1)}, u32[]{:S(2)}, u32[]{:S(2)}) %collective-permute-start.30) | collective-permute-done | bytes 86048 | tf_op jit(solution)/shard_map/ppermute | solution.py:19
  61.3 1.9 %collective-permute-start.31 = (bf16[112,384]{1,0:T(8,128)(2,1)S(1)}, bf16[112,384]{1,0:T(8,128)(2,1)S(1)}, u32[]{:S(2)}, u32[]{:S(2)}) collective-permute-start(bf16[112,384]{1,0:T(8,128)(2,1)S(1)} %get-tuple-element.34), channel_id=1, source_target_pairs={{0,4},{4,0},{8,12},{12,8},{16,20},{20,16},{24,28},{28,24},{1,5},{5... | collective-permute-start | bytes 258056 | tf_op jit(solution)/shard_map/ppermute | solution.py:19
  63.3 1.9 %collective-permute-start.12 = (bf16[112,384]{1,0:T(8,128)(2,1)S(1)}, bf16[112,384]{1,0:T(8,128)(2,1)S(1)}, u32[]{:S(2)}, u32[]{:S(2)}) collective-permute-start(bf16[112,384]{1,0:T(8,128)(2,1)S(1)} %get-tuple-element.35), channel_id=1, source_target_pairs={{0,8},{4,12},{8,0},{12,4},{16,24},{20,28},{24,16},{28,20},{1,9},{5... | collective-permute-start | bytes 258056 | tf_op jit(solution)/shard_map/ppermute | solution.py:19
  65.7 1.0 %collective-permute-done.38 = bf16[112,384]{1,0:T(8,128)(2,1)S(1)} collective-permute-done((bf16[112,384]{1,0:T(8,128)(2,1)S(1)}, bf16[112,384]{1,0:T(8,128)(2,1)S(1)}, u32[]{:S(2)}, u32[]{:S(2)}) %collective-permute-start.38) | collective-permute-done | bytes 86048 | tf_op jit(solution)/shard_map/ppermute | solution.py:19
  66.7 1.9 %collective-permute-start.20 = (bf16[112,384]{1,0:T(8,128)(2,1)S(1)}, bf16[112,384]{1,0:T(8,128)(2,1)S(1)}, u32[]{:S(2)}, u32[]{:S(2)}) collective-permute-start(bf16[112,384]{1,0:T(8,128)(2,1)S(1)} %get-tuple-element.38), channel_id=1, source_target_pairs={{0,4},{4,0},{8,12},{12,8},{16,20},{20,16},{24,28},{28,24},{1,5},{5... | collective-permute-start | bytes 258056 | tf_op jit(solution)/shard_map/ppermute | solution.py:19
  68.9 1.8 %collective-permute-start.32 = (bf16[2,112,384]{2,1,0:T(8,128)(2,1)S(1)}, bf16[2,112,384]{2,1,0:T(8,128)(2,1)S(1)}, u32[]{:S(2)}, u32[]{:S(2)}) collective-permute-start(bf16[2,112,384]{2,1,0:T(8,128)(2,1)S(1)} %maximum_select_fusion.10), channel_id=1, source_target_pairs={{0,8},{4,12},{8,0},{12,4},{16,24},{20,28},{24,16},{28,20},{1,9},{5... | collective-permute-start | bytes 516104 | tf_op jit(solution)/shard_map/ppermute | solution.py:19
  70.8 1.1 %collective-permute-start.13 = (bf16[2,112,384]{2,1,0:T(8,128)(2,1)S(1)}, bf16[2,112,384]{2,1,0:T(8,128)(2,1)S(1)}, u32[]{:S(2)}, u32[]{:S(2)}) collective-permute-start(bf16[2,112,384]{2,1,0:T(8,128)(2,1)S(1)} %maximum_select_fusion.6), channel_id=1, source_target_pairs={{0,4},{4,0},{8,12},{12,8},{16,20},{20,16},{24,28},{28,24},{1,5},{5... | collective-permute-start | bytes 516104 | tf_op jit(solution)/shard_map/ppermute | solution.py:19
  71.9 1.2 %collective-permute-start.41 = (bf16[2,112,384]{2,1,0:T(8,128)(2,1)S(1)}, bf16[2,112,384]{2,1,0:T(8,128)(2,1)S(1)}, u32[]{:S(2)}, u32[]{:S(2)}) collective-permute-start(bf16[2,112,384]{2,1,0:T(8,128)(2,1)S(1)} %maximum_select_fusion.16), channel_id=1, source_target_pairs={{0,8},{4,12},{8,0},{12,4},{16,24},{20,28},{24,16},{28,20},{1,9},{5... | collective-permute-start | bytes 516104 | tf_op jit(solution)/shard_map/ppermute | solution.py:19
  73.2 1.0 collective-permute-start.21
  74.3 2.0 %collective-permute-done.13 = bf16[2,112,384]{2,1,0:T(8,128)(2,1)S(1)} collective-permute-done((bf16[2,112,384]{2,1,0:T(8,128)(2,1)S(1)}, bf16[2,112,384]{2,1,0:T(8,128)(2,1)S(1)}, u32[]{:S(2)}, u32[]{:S(2)}) %collective-permute-start.13) | collective-permute-done | bytes 172064 | tf_op jit(solution)/shard_map/ppermute | solution.py:19
  76.3 1.0 %collective-permute-start.37 = (bf16[2,112,384]{2,1,0:T(8,128)(2,1)S(1)}, bf16[2,112,384]{2,1,0:T(8,128)(2,1)S(1)}, u32[]{:S(2)}, u32[]{:S(2)}) collective-permute-start(bf16[2,112,384]{2,1,0:T(8,128)(2,1)S(1)} %maximum_select_fusion.12), channel_id=1, source_target_pairs={{0,4},{4,0},{8,12},{12,8},{16,20},{20,16},{24,28},{28,24},{1,5},{5... | collective-permute-start | bytes 516104 | tf_op jit(solution)/shard_map/ppermute | solution.py:19
  77.3 1.9 %collective-permute-done.21 = bf16[2,112,384]{2,1,0:T(8,128)(2,1)S(1)} collective-permute-done((bf16[2,112,384]{2,1,0:T(8,128)(2,1)S(1)}, bf16[2,112,384]{2,1,0:T(8,128)(2,1)S(1)}, u32[]{:S(2)}, u32[]{:S(2)}) %collective-permute-start.21) | collective-permute-done | bytes 172064 | tf_op jit(solution)/shard_map/ppermute | solution.py:19
  80.6 1.1 %collective-permute-done.37 = bf16[2,112,384]{2,1,0:T(8,128)(2,1)S(1)} collective-permute-done((bf16[2,112,384]{2,1,0:T(8,128)(2,1)S(1)}, bf16[2,112,384]{2,1,0:T(8,128)(2,1)S(1)}, u32[]{:S(2)}, u32[]{:S(2)}) %collective-permute-start.37) | collective-permute-done | bytes 172064 | tf_op jit(solution)/shard_map/ppermute | solution.py:19
  84.0 1.6 %collective-permute-start.44 = (bf16[2,56,512]{2,1,0:T(8,128)(2,1)S(1)}, bf16[2,56,512]{2,1,0:T(8,128)(2,1)S(1)}, u32[]{:S(2)}, u32[]{:S(2)}) collective-permute-start(bf16[2,56,512]{2,1,0:T(8,128)(2,1)S(1)} %get-tuple-element.27), channel_id=1, source_target_pairs={{0,3},{1,2},{2,1},{3,0},{4,7},{5,6},{6,5},{7,4},{8,11},{9,10},{10,... | collective-permute-start | bytes 344072 | tf_op jit(solution)/shard_map/ppermute | solution.py:19
  85.6 1.8 %convolution_convert_fusion = bf16[2,768,512]{2,1,0:T(8,128)(2,1)} fusion(bf16[2,224,768]{2,1,0:T(8,128)(2,1)S(1)} %pad_maximum_fusion, bf16[2,224,512]{2,1,0:T(8,128)(2,1)S(1)} %bitcast.267), kind=kOutput, calls=%fused_computation | convolution fusion | flops 353107968 | bytes 2719744 | tf_op jit(solution)/shard_map/jrf,jrd->jfd/dot_general | solution.py:107
  87.4 1.8 %convolution_convert_fusion.2 = bf16[2,512,768]{2,1,0:T(8,128)(2,1)} fusion(bf16[2,224,512]{2,1,0:T(8,128)(2,1)S(1)} %bitcast.264, bf16[2,224,768]{2,1,0:T(8,128)(2,1)S(1)} %pad_maximum_fusion.1), kind=kOutput, calls=%fused_computation.2 | convolution fusion | flops 353107968 | bytes 2719744 | tf_op jit(solution)/shard_map/jrd,jrf->jdf/dot_general | solution.py:107
  89.2 1.8 %convolution_convert_fusion.1 = bf16[2,512,768]{2,1,0:T(8,128)(2,1)} fusion(bf16[2,224,512]{2,1,0:T(8,128)(2,1)S(1)} %bitcast.265, bf16[2,224,768]{2,1,0:T(8,128)(2,1)S(1)} %pad_maximum_fusion.2), kind=kOutput, calls=%fused_computation.1 | convolution fusion | flops 353107968 | bytes 2719744 | tf_op jit(solution)/shard_map/jrd,jrf->jdf/dot_general | solution.py:107
  91.6 1.0 %fusion.1 = bf16[128,512]{1,0:T(8,128)(2,1)} fusion(bf16[448,512,1]{1,0,2:T(8,128)(2,1)S(1)} %bitcast.306, f32[2,128]{1,0:T(2,128)S(1)} %bitcast.333, s32[2,128]{1,0:T(2,128)S(1)} %multiply_add_fusion), kind=kOutput, calls=%fused_computation.10 | convolution fusion | flops 117751808 | bytes 591872 | tf_op jit(solution)/shard_map/ktr,rd->ktd/dot_general | solution.py:107
  92.6 3.5 %collective-permute-done.43 = bf16[2,56,512]{2,1,0:T(8,128)(2,1)S(1)} collective-permute-done((bf16[2,56,512]{2,1,0:T(8,128)(2,1)S(1)}, bf16[2,56,512]{2,1,0:T(8,128)(2,1)S(1)}, u32[]{:S(2)}, u32[]{:S(2)}) %collective-permute-start.43) | collective-permute-done | bytes 114720 | tf_op jit(solution)/shard_map/ppermute | solution.py:19
  96.2 0.9 convolution_convert_fusion.7
  (148 shorter events, 13.1 us)
Async XLA Ops:
  0.6 21.2 %copy-start = (bf16[2,768,512]{2,1,0:T(8,128)(2,1)S(1)}, bf16[2,768,512]{2,1,0:T(8,128)(2,1)}, u32[]{:S(2)}) copy-start(bf16[2,768,512]{2,1,0:T(8,128)(2,1)} %param.13) | copy-start | bytes 4718596
  2.1 5.9 %collective-permute-start.1 = (f32[4,128]{1,0:T(4,128)S(1)}, f32[4,128]{1,0:T(4,128)S(1)}, u32[]{:S(2)}, u32[]{:S(2)}) collective-permute-start(f32[4,128]{1,0:T(4,128)S(1)} %pad_maximum_fusion.8), channel_id=1, source_target_pairs={{0,2},{1,3},{2,0},{3,1},{4,6},{5,7},{6,4},{7,5},{8,10},{9,11},{10,... | collective-permute-start | bytes 6152 | tf_op jit(solution)/shard_map/ppermute | solution.py:19
  5.1 3.4 %collective-permute-start = (f32[4,128]{1,0:T(4,128)S(1)}, f32[4,128]{1,0:T(4,128)S(1)}, u32[]{:S(2)}, u32[]{:S(2)}) collective-permute-start(f32[4,128]{1,0:T(4,128)S(1)} %pad_maximum_fusion.8), channel_id=1, source_target_pairs={{0,1},{1,0},{2,3},{3,2},{4,5},{5,4},{6,7},{7,6},{8,9},{9,8},{10,11... | collective-permute-start | bytes 6152 | tf_op jit(solution)/shard_map/ppermute | solution.py:19
  5.1 6.1 %collective-permute-start.4 = (bf16[128,512]{1,0:T(8,128)(2,1)}, bf16[128,512]{1,0:T(8,128)(2,1)S(1)}, u32[]{:S(2)}, u32[]{:S(2)}) collective-permute-start(bf16[128,512]{1,0:T(8,128)(2,1)} %param.7), channel_id=1, source_target_pairs={{0,2},{1,3},{2,0},{3,1},{4,6},{5,7},{6,4},{7,5},{8,10},{9,11},{10,... | collective-permute-start | bytes 393224 | tf_op jit(solution)/shard_map/ppermute | solution.py:19
  5.2 7.9 %collective-permute-start.3 = (bf16[128,512]{1,0:T(8,128)(2,1)}, bf16[128,512]{1,0:T(8,128)(2,1)S(1)}, u32[]{:S(2)}, u32[]{:S(2)}) collective-permute-start(bf16[128,512]{1,0:T(8,128)(2,1)} %param.7), channel_id=1, source_target_pairs={{0,1},{1,0},{2,3},{3,2},{4,5},{5,4},{6,7},{7,6},{8,9},{9,8},{10,11... | collective-permute-start | bytes 393224 | tf_op jit(solution)/shard_map/ppermute | solution.py:19
  5.6 14.7 %collective-permute-start.25 = (bf16[128,512]{1,0:T(8,128)(2,1)}, bf16[128,512]{1,0:T(8,128)(2,1)S(1)}, u32[]{:S(2)}, u32[]{:S(2)}) collective-permute-start(bf16[128,512]{1,0:T(8,128)(2,1)} %param.8), channel_id=1, source_target_pairs={{0,1},{1,0},{2,3},{3,2},{4,5},{5,4},{6,7},{7,6},{8,9},{9,8},{10,11... | collective-permute-start | bytes 393224 | tf_op jit(solution)/shard_map/ppermute | solution.py:19
  8.1 1.3 %collective-permute-start.2 = (f32[4,128]{1,0:T(4,128)S(1)}, f32[4,128]{1,0:T(4,128)S(1)}, u32[]{:S(2)}, u32[]{:S(2)}) collective-permute-start(f32[4,128]{1,0:T(4,128)S(1)} %collective-permute-done.1), channel_id=1, source_target_pairs={{0,1},{1,0},{2,3},{3,2},{4,5},{5,4},{6,7},{7,6},{8,9},{9,8},{10,11... | collective-permute-start | bytes 6152 | tf_op jit(solution)/shard_map/ppermute | solution.py:19
  9.3 5.2 %copy-start.1 = (bf16[2,512,768]{2,1,0:T(8,128)(2,1)S(1)}, bf16[2,512,768]{2,1,0:T(8,128)(2,1)}, u32[]{:S(2)}) copy-start(bf16[2,512,768]{2,1,0:T(8,128)(2,1)} %param.12) | copy-start | bytes 4718596
  11.2 8.9 %collective-permute-start.26 = (bf16[128,512]{1,0:T(8,128)(2,1)}, bf16[128,512]{1,0:T(8,128)(2,1)S(1)}, u32[]{:S(2)}, u32[]{:S(2)}) collective-permute-start(bf16[128,512]{1,0:T(8,128)(2,1)} %param.8), channel_id=1, source_target_pairs={{0,2},{1,3},{2,0},{3,1},{4,6},{5,7},{6,4},{7,5},{8,10},{9,11},{10,... | collective-permute-start | bytes 393224 | tf_op jit(solution)/shard_map/ppermute | solution.py:19
  12.9 1.3 %collective-permute-start.5 = (bf16[128,512]{1,0:T(8,128)(2,1)S(1)}, bf16[128,512]{1,0:T(8,128)(2,1)S(1)}, u32[]{:S(2)}, u32[]{:S(2)}) collective-permute-start(bf16[128,512]{1,0:T(8,128)(2,1)S(1)} %collective-permute-done.4), channel_id=1, source_target_pairs={{0,1},{1,0},{2,3},{3,2},{4,5},{5,4},{6,7},{7,6},{8,9},{9,8},{10,11... | collective-permute-start | bytes 393224 | tf_op jit(solution)/shard_map/ppermute | solution.py:19
  15.1 3.4 %copy-start.2 = (bf16[2,512,768]{2,1,0:T(8,128)(2,1)S(1)}, bf16[2,512,768]{2,1,0:T(8,128)(2,1)}, u32[]{:S(2)}) copy-start(bf16[2,512,768]{2,1,0:T(8,128)(2,1)} %param.11) | copy-start | bytes 4718596
  15.2 8.8 %collective-permute-start.9 = (bf16[2,112,384]{2,1,0:T(8,128)(2,1)S(1)}, bf16[2,112,384]{2,1,0:T(8,128)(2,1)S(1)}, u32[]{:S(2)}, u32[]{:S(2)}) collective-permute-start(bf16[2,112,384]{2,1,0:T(8,128)(2,1)S(1)} %dynamic-slice_bitcast_fusion.4), channel_id=1, source_target_pairs={{0,8},{4,12},{8,0},{12,4},{16,24},{20,28},{24,16},{28,20},{1,9},{5... | collective-permute-start | bytes 516104 | tf_op jit(solution)/shard_map/ppermute | solution.py:19
  16.9 8.4 %collective-permute-start.17 = (bf16[2,112,384]{2,1,0:T(8,128)(2,1)S(1)}, bf16[2,112,384]{2,1,0:T(8,128)(2,1)S(1)}, u32[]{:S(2)}, u32[]{:S(2)}) collective-permute-start(bf16[2,112,384]{2,1,0:T(8,128)(2,1)S(1)} %dynamic-slice_bitcast_fusion.2), channel_id=1, source_target_pairs={{0,4},{4,0},{8,12},{12,8},{16,20},{20,16},{24,28},{28,24},{1,5},{5... | collective-permute-start | bytes 516104 | tf_op jit(solution)/shard_map/ppermute | solution.py:19
  19.2 8.7 %collective-permute-start.6 = (bf16[2,112,384]{2,1,0:T(8,128)(2,1)S(1)}, bf16[2,112,384]{2,1,0:T(8,128)(2,1)S(1)}, u32[]{:S(2)}, u32[]{:S(2)}) collective-permute-start(bf16[2,112,384]{2,1,0:T(8,128)(2,1)S(1)} %dynamic-slice_bitcast_fusion.5), channel_id=1, source_target_pairs={{0,4},{4,0},{8,12},{12,8},{16,20},{20,16},{24,28},{28,24},{1,5},{5... | collective-permute-start | bytes 516104 | tf_op jit(solution)/shard_map/ppermute | solution.py:19
  20.1 1.4 %collective-permute-start.27 = (bf16[128,512]{1,0:T(8,128)(2,1)S(1)}, bf16[128,512]{1,0:T(8,128)(2,1)S(1)}, u32[]{:S(2)}, u32[]{:S(2)}) collective-permute-start(bf16[128,512]{1,0:T(8,128)(2,1)S(1)} %collective-permute-done.26), channel_id=1, source_target_pairs={{0,1},{1,0},{2,3},{3,2},{4,5},{5,4},{6,7},{7,6},{8,9},{9,8},{10,11... | collective-permute-start | bytes 393224 | tf_op jit(solution)/shard_map/ppermute | solution.py:19
  20.4 7.6 %collective-permute-start.14 = (bf16[2,112,384]{2,1,0:T(8,128)(2,1)S(1)}, bf16[2,112,384]{2,1,0:T(8,128)(2,1)S(1)}, u32[]{:S(2)}, u32[]{:S(2)}) collective-permute-start(bf16[2,112,384]{2,1,0:T(8,128)(2,1)S(1)} %dynamic-slice_bitcast_fusion.3), channel_id=1, source_target_pairs={{0,8},{4,12},{8,0},{12,4},{16,24},{20,28},{24,16},{28,20},{1,9},{5... | collective-permute-start | bytes 516104 | tf_op jit(solution)/shard_map/ppermute | solution.py:19
  22.6 17.1 %collective-permute-start.28 = (bf16[2,112,384]{2,1,0:T(8,128)(2,1)S(1)}, bf16[2,112,384]{2,1,0:T(8,128)(2,1)S(1)}, u32[]{:S(2)}, u32[]{:S(2)}) collective-permute-start(bf16[2,112,384]{2,1,0:T(8,128)(2,1)S(1)} %dynamic-slice_bitcast_fusion.1), channel_id=1, source_target_pairs={{0,4},{4,0},{8,12},{12,8},{16,20},{20,16},{24,28},{28,24},{1,5},{5... | collective-permute-start | bytes 516104 | tf_op jit(solution)/shard_map/ppermute | solution.py:19
  24.0 16.7 %collective-permute-start.33 = (bf16[2,112,384]{2,1,0:T(8,128)(2,1)S(1)}, bf16[2,112,384]{2,1,0:T(8,128)(2,1)S(1)}, u32[]{:S(2)}, u32[]{:S(2)}) collective-permute-start(bf16[2,112,384]{2,1,0:T(8,128)(2,1)S(1)} %dynamic-slice_bitcast_fusion), channel_id=1, source_target_pairs={{0,8},{4,12},{8,0},{12,4},{16,24},{20,28},{24,16},{28,20},{1,9},{5... | collective-permute-start | bytes 516104 | tf_op jit(solution)/shard_map/ppermute | solution.py:19
  25.3 7.0 %collective-permute-start.10 = (bf16[112,384]{1,0:T(8,128)(2,1)S(1)}, bf16[112,384]{1,0:T(8,128)(2,1)S(1)}, u32[]{:S(2)}, u32[]{:S(2)}) collective-permute-start(bf16[112,384]{1,0:T(8,128)(2,1)S(1)} %fusion.35), channel_id=1, source_target_pairs={{0,4},{4,0},{8,12},{12,8},{16,20},{20,16},{24,28},{28,24},{1,5},{5... | collective-permute-start | bytes 258056 | tf_op jit(solution)/shard_map/ppermute | solution.py:19
  27.9 6.0 %collective-permute-start.18 = (bf16[112,384]{1,0:T(8,128)(2,1)S(1)}, bf16[112,384]{1,0:T(8,128)(2,1)S(1)}, u32[]{:S(2)}, u32[]{:S(2)}) collective-permute-start(bf16[112,384]{1,0:T(8,128)(2,1)S(1)} %fusion.37), channel_id=1, source_target_pairs={{0,8},{4,12},{8,0},{12,4},{16,24},{20,28},{24,16},{28,20},{1,9},{5... | collective-permute-start | bytes 258056 | tf_op jit(solution)/shard_map/ppermute | solution.py:19
  28.0 8.6 %collective-permute-start.7 = (bf16[112,384]{1,0:T(8,128)(2,1)S(1)}, bf16[112,384]{1,0:T(8,128)(2,1)S(1)}, u32[]{:S(2)}, u32[]{:S(2)}) collective-permute-start(bf16[112,384]{1,0:T(8,128)(2,1)S(1)} %fusion.34), channel_id=1, source_target_pairs={{0,8},{4,12},{8,0},{12,4},{16,24},{20,28},{24,16},{28,20},{1,9},{5... | collective-permute-start | bytes 258056 | tf_op jit(solution)/shard_map/ppermute | solution.py:19
  32.3 5.2 %collective-permute-start.15 = (bf16[112,384]{1,0:T(8,128)(2,1)S(1)}, bf16[112,384]{1,0:T(8,128)(2,1)S(1)}, u32[]{:S(2)}, u32[]{:S(2)}) collective-permute-start(bf16[112,384]{1,0:T(8,128)(2,1)S(1)} %fusion.36), channel_id=1, source_target_pairs={{0,4},{4,0},{8,12},{12,8},{16,20},{20,16},{24,28},{28,24},{1,5},{5... | collective-permute-start | bytes 258056 | tf_op jit(solution)/shard_map/ppermute | solution.py:19
  33.9 20.8 %collective-permute-start.11 = (bf16[112,384]{1,0:T(8,128)(2,1)S(1)}, bf16[112,384]{1,0:T(8,128)(2,1)S(1)}, u32[]{:S(2)}, u32[]{:S(2)}) collective-permute-start(bf16[112,384]{1,0:T(8,128)(2,1)S(1)} %fusion.22), channel_id=1, source_target_pairs={{0,16},{4,20},{8,24},{12,28},{16,0},{20,4},{24,8},{28,12},{1,17},{... | collective-permute-start | bytes 258056 | tf_op jit(solution)/shard_map/ppermute | solution.py:19
  36.6 26.7 %collective-permute-start.19 = (bf16[112,384]{1,0:T(8,128)(2,1)S(1)}, bf16[112,384]{1,0:T(8,128)(2,1)S(1)}, u32[]{:S(2)}, u32[]{:S(2)}) collective-permute-start(bf16[112,384]{1,0:T(8,128)(2,1)S(1)} %fusion.20), channel_id=1, source_target_pairs={{0,16},{4,20},{8,24},{12,28},{16,0},{20,4},{24,8},{28,12},{1,17},{... | collective-permute-start | bytes 258056 | tf_op jit(solution)/shard_map/ppermute | solution.py:19
  37.5 20.2 %collective-permute-start.8 = (bf16[112,384]{1,0:T(8,128)(2,1)S(1)}, bf16[112,384]{1,0:T(8,128)(2,1)S(1)}, u32[]{:S(2)}, u32[]{:S(2)}) collective-permute-start(bf16[112,384]{1,0:T(8,128)(2,1)S(1)} %fusion.23), channel_id=1, source_target_pairs={{0,16},{4,20},{8,24},{12,28},{16,0},{20,4},{24,8},{28,12},{1,17},{... | collective-permute-start | bytes 258056 | tf_op jit(solution)/shard_map/ppermute | solution.py:19
  39.7 25.5 %collective-permute-start.16 = (bf16[112,384]{1,0:T(8,128)(2,1)S(1)}, bf16[112,384]{1,0:T(8,128)(2,1)S(1)}, u32[]{:S(2)}, u32[]{:S(2)}) collective-permute-start(bf16[112,384]{1,0:T(8,128)(2,1)S(1)} %fusion.21), channel_id=1, source_target_pairs={{0,16},{4,20},{8,24},{12,28},{16,0},{20,4},{24,8},{28,12},{1,17},{... | collective-permute-start | bytes 258056 | tf_op jit(solution)/shard_map/ppermute | solution.py:19
  40.7 4.9 %collective-permute-start.29 = (bf16[112,384]{1,0:T(8,128)(2,1)S(1)}, bf16[112,384]{1,0:T(8,128)(2,1)S(1)}, u32[]{:S(2)}, u32[]{:S(2)}) collective-permute-start(bf16[112,384]{1,0:T(8,128)(2,1)S(1)} %fusion.38), channel_id=1, source_target_pairs={{0,8},{4,12},{8,0},{12,4},{16,24},{20,28},{24,16},{28,20},{1,9},{5... | collective-permute-start | bytes 258056 | tf_op jit(solution)/shard_map/ppermute | solution.py:19
  45.5 9.1 %collective-permute-start.34 = (bf16[112,384]{1,0:T(8,128)(2,1)S(1)}, bf16[112,384]{1,0:T(8,128)(2,1)S(1)}, u32[]{:S(2)}, u32[]{:S(2)}) collective-permute-start(bf16[112,384]{1,0:T(8,128)(2,1)S(1)} %fusion.39), channel_id=1, source_target_pairs={{0,4},{4,0},{8,12},{12,8},{16,20},{20,16},{24,28},{28,24},{1,5},{5... | collective-permute-start | bytes 258056 | tf_op jit(solution)/shard_map/ppermute | solution.py:19
  54.6 6.5 %collective-permute-start.30 = (bf16[112,384]{1,0:T(8,128)(2,1)S(1)}, bf16[112,384]{1,0:T(8,128)(2,1)S(1)}, u32[]{:S(2)}, u32[]{:S(2)}) collective-permute-start(bf16[112,384]{1,0:T(8,128)(2,1)S(1)} %fusion.19), channel_id=1, source_target_pairs={{0,16},{4,20},{8,24},{12,28},{16,0},{20,4},{24,8},{28,12},{1,17},{... | collective-permute-start | bytes 258056 | tf_op jit(solution)/shard_map/ppermute | solution.py:19
  54.7 10.5 %collective-permute-start.35 = (bf16[112,384]{1,0:T(8,128)(2,1)S(1)}, bf16[112,384]{1,0:T(8,128)(2,1)S(1)}, u32[]{:S(2)}, u32[]{:S(2)}) collective-permute-start(bf16[112,384]{1,0:T(8,128)(2,1)S(1)} %fusion.18), channel_id=1, source_target_pairs={{0,16},{4,20},{8,24},{12,28},{16,0},{20,4},{24,8},{28,12},{1,17},{... | collective-permute-start | bytes 258056 | tf_op jit(solution)/shard_map/ppermute | solution.py:19
  61.3 5.5 %collective-permute-start.38 = (bf16[112,384]{1,0:T(8,128)(2,1)S(1)}, bf16[112,384]{1,0:T(8,128)(2,1)S(1)}, u32[]{:S(2)}, u32[]{:S(2)}) collective-permute-start(bf16[112,384]{1,0:T(8,128)(2,1)S(1)} %get-tuple-element.33), channel_id=1, source_target_pairs={{0,8},{4,12},{8,0},{12,4},{16,24},{20,28},{24,16},{28,20},{1,9},{5... | collective-permute-start | bytes 258056 | tf_op jit(solution)/shard_map/ppermute | solution.py:19
  61.3 7.3 %collective-permute-start.31 = (bf16[112,384]{1,0:T(8,128)(2,1)S(1)}, bf16[112,384]{1,0:T(8,128)(2,1)S(1)}, u32[]{:S(2)}, u32[]{:S(2)}) collective-permute-start(bf16[112,384]{1,0:T(8,128)(2,1)S(1)} %get-tuple-element.34), channel_id=1, source_target_pairs={{0,4},{4,0},{8,12},{12,8},{16,20},{20,16},{24,28},{28,24},{1,5},{5... | collective-permute-start | bytes 258056 | tf_op jit(solution)/shard_map/ppermute | solution.py:19
  63.3 5.6 %collective-permute-start.12 = (bf16[112,384]{1,0:T(8,128)(2,1)S(1)}, bf16[112,384]{1,0:T(8,128)(2,1)S(1)}, u32[]{:S(2)}, u32[]{:S(2)}) collective-permute-start(bf16[112,384]{1,0:T(8,128)(2,1)S(1)} %get-tuple-element.35), channel_id=1, source_target_pairs={{0,8},{4,12},{8,0},{12,4},{16,24},{20,28},{24,16},{28,20},{1,9},{5... | collective-permute-start | bytes 258056 | tf_op jit(solution)/shard_map/ppermute | solution.py:19
  65.4 5.4 %collective-permute-start.40 = (bf16[112,384]{1,0:T(8,128)(2,1)S(1)}, bf16[112,384]{1,0:T(8,128)(2,1)S(1)}, u32[]{:S(2)}, u32[]{:S(2)}) collective-permute-start(bf16[112,384]{1,0:T(8,128)(2,1)S(1)} %get-tuple-element.36), channel_id=1, source_target_pairs={{0,4},{4,0},{8,12},{12,8},{16,20},{20,16},{24,28},{28,24},{1,5},{5... | collective-permute-start | bytes 258056 | tf_op jit(solution)/shard_map/ppermute | solution.py:19
  65.6 7.6 %collective-permute-start.36 = (bf16[112,384]{1,0:T(8,128)(2,1)S(1)}, bf16[112,384]{1,0:T(8,128)(2,1)S(1)}, u32[]{:S(2)}, u32[]{:S(2)}) collective-permute-start(bf16[112,384]{1,0:T(8,128)(2,1)S(1)} %get-tuple-element.37), channel_id=1, source_target_pairs={{0,8},{4,12},{8,0},{12,4},{16,24},{20,28},{24,16},{28,20},{1,9},{5... | collective-permute-start | bytes 258056 | tf_op jit(solution)/shard_map/ppermute | solution.py:19
  66.7 5.2 %collective-permute-start.20 = (bf16[112,384]{1,0:T(8,128)(2,1)S(1)}, bf16[112,384]{1,0:T(8,128)(2,1)S(1)}, u32[]{:S(2)}, u32[]{:S(2)}) collective-permute-start(bf16[112,384]{1,0:T(8,128)(2,1)S(1)} %get-tuple-element.38), channel_id=1, source_target_pairs={{0,4},{4,0},{8,12},{12,8},{16,20},{20,16},{24,28},{28,24},{1,5},{5... | collective-permute-start | bytes 258056 | tf_op jit(solution)/shard_map/ppermute | solution.py:19
  68.6 14.5 %collective-permute-start.39 = (bf16[2,112,384]{2,1,0:T(8,128)(2,1)S(1)}, bf16[2,112,384]{2,1,0:T(8,128)(2,1)S(1)}, u32[]{:S(2)}, u32[]{:S(2)}) collective-permute-start(bf16[2,112,384]{2,1,0:T(8,128)(2,1)S(1)} %maximum_select_fusion.14), channel_id=1, source_target_pairs={{0,4},{4,0},{8,12},{12,8},{16,20},{20,16},{24,28},{28,24},{1,5},{5... | collective-permute-start | bytes 516104 | tf_op jit(solution)/shard_map/ppermute | solution.py:19
  68.9 11.0 %collective-permute-start.32 = (bf16[2,112,384]{2,1,0:T(8,128)(2,1)S(1)}, bf16[2,112,384]{2,1,0:T(8,128)(2,1)S(1)}, u32[]{:S(2)}, u32[]{:S(2)}) collective-permute-start(bf16[2,112,384]{2,1,0:T(8,128)(2,1)S(1)} %maximum_select_fusion.10), channel_id=1, source_target_pairs={{0,8},{4,12},{8,0},{12,4},{16,24},{20,28},{24,16},{28,20},{1,9},{5... | collective-permute-start | bytes 516104 | tf_op jit(solution)/shard_map/ppermute | solution.py:19
  70.8 5.5 %collective-permute-start.13 = (bf16[2,112,384]{2,1,0:T(8,128)(2,1)S(1)}, bf16[2,112,384]{2,1,0:T(8,128)(2,1)S(1)}, u32[]{:S(2)}, u32[]{:S(2)}) collective-permute-start(bf16[2,112,384]{2,1,0:T(8,128)(2,1)S(1)} %maximum_select_fusion.6), channel_id=1, source_target_pairs={{0,4},{4,0},{8,12},{12,8},{16,20},{20,16},{24,28},{28,24},{1,5},{5... | collective-permute-start | bytes 516104 | tf_op jit(solution)/shard_map/ppermute | solution.py:19
  71.9 11.1 %collective-permute-start.41 = (bf16[2,112,384]{2,1,0:T(8,128)(2,1)S(1)}, bf16[2,112,384]{2,1,0:T(8,128)(2,1)S(1)}, u32[]{:S(2)}, u32[]{:S(2)}) collective-permute-start(bf16[2,112,384]{2,1,0:T(8,128)(2,1)S(1)} %maximum_select_fusion.16), channel_id=1, source_target_pairs={{0,8},{4,12},{8,0},{12,4},{16,24},{20,28},{24,16},{28,20},{1,9},{5... | collective-permute-start | bytes 516104 | tf_op jit(solution)/shard_map/ppermute | solution.py:19
  73.2 6.1 %collective-permute-start.21 = (bf16[2,112,384]{2,1,0:T(8,128)(2,1)S(1)}, bf16[2,112,384]{2,1,0:T(8,128)(2,1)S(1)}, u32[]{:S(2)}, u32[]{:S(2)}) collective-permute-start(bf16[2,112,384]{2,1,0:T(8,128)(2,1)S(1)} %maximum_select_fusion.8), channel_id=1, source_target_pairs={{0,8},{4,12},{8,0},{12,4},{16,24},{20,28},{24,16},{28,20},{1,9},{5... | collective-permute-start | bytes 516104 | tf_op jit(solution)/shard_map/ppermute | solution.py:19
  76.3 5.4 %collective-permute-start.37 = (bf16[2,112,384]{2,1,0:T(8,128)(2,1)S(1)}, bf16[2,112,384]{2,1,0:T(8,128)(2,1)S(1)}, u32[]{:S(2)}, u32[]{:S(2)}) collective-permute-start(bf16[2,112,384]{2,1,0:T(8,128)(2,1)S(1)} %maximum_select_fusion.12), channel_id=1, source_target_pairs={{0,4},{4,0},{8,12},{12,8},{16,20},{20,16},{24,28},{28,24},{1,5},{5... | collective-permute-start | bytes 516104 | tf_op jit(solution)/shard_map/ppermute | solution.py:19
  79.8 11.1 %collective-permute-start.22 = (bf16[2,56,512]{2,1,0:T(8,128)(2,1)S(1)}, bf16[2,56,512]{2,1,0:T(8,128)(2,1)S(1)}, u32[]{:S(2)}, u32[]{:S(2)}) collective-permute-start(bf16[2,56,512]{2,1,0:T(8,128)(2,1)S(1)} %get-tuple-element.30), channel_id=1, source_target_pairs={{0,1},{1,0},{2,3},{3,2},{4,5},{5,4},{6,7},{7,6},{8,9},{9,8},{10,11... | collective-permute-start | bytes 344072 | tf_op jit(solution)/shard_map/ppermute | solution.py:19
  79.9 11.6 %collective-permute-start.24 = (bf16[2,56,512]{2,1,0:T(8,128)(2,1)S(1)}, bf16[2,56,512]{2,1,0:T(8,128)(2,1)S(1)}, u32[]{:S(2)}, u32[]{:S(2)}) collective-permute-start(bf16[2,56,512]{2,1,0:T(8,128)(2,1)S(1)} %get-tuple-element.31), channel_id=1, source_target_pairs={{0,3},{1,2},{2,1},{3,0},{4,7},{5,6},{6,5},{7,4},{8,11},{9,10},{10,... | collective-permute-start | bytes 344072 | tf_op jit(solution)/shard_map/ppermute | solution.py:19
  81.7 9.8 %collective-permute-start.23 = (bf16[2,56,512]{2,1,0:T(8,128)(2,1)S(1)}, bf16[2,56,512]{2,1,0:T(8,128)(2,1)S(1)}, u32[]{:S(2)}, u32[]{:S(2)}) collective-permute-start(bf16[2,56,512]{2,1,0:T(8,128)(2,1)S(1)} %get-tuple-element.32), channel_id=1, source_target_pairs={{0,2},{1,3},{2,0},{3,1},{4,6},{5,7},{6,4},{7,5},{8,10},{9,11},{10,... | collective-permute-start | bytes 344072 | tf_op jit(solution)/shard_map/ppermute | solution.py:19
  84.0 8.6 %collective-permute-start.42 = (bf16[2,56,512]{2,1,0:T(8,128)(2,1)S(1)}, bf16[2,56,512]{2,1,0:T(8,128)(2,1)S(1)}, u32[]{:S(2)}, u32[]{:S(2)}) collective-permute-start(bf16[2,56,512]{2,1,0:T(8,128)(2,1)S(1)} %get-tuple-element.26), channel_id=1, source_target_pairs={{0,1},{1,0},{2,3},{3,2},{4,5},{5,4},{6,7},{7,6},{8,9},{9,8},{10,11... | collective-permute-start | bytes 344072 | tf_op jit(solution)/shard_map/ppermute | solution.py:19
  84.0 8.5 %collective-permute-start.44 = (bf16[2,56,512]{2,1,0:T(8,128)(2,1)S(1)}, bf16[2,56,512]{2,1,0:T(8,128)(2,1)S(1)}, u32[]{:S(2)}, u32[]{:S(2)}) collective-permute-start(bf16[2,56,512]{2,1,0:T(8,128)(2,1)S(1)} %get-tuple-element.27), channel_id=1, source_target_pairs={{0,3},{1,2},{2,1},{3,0},{4,7},{5,6},{6,5},{7,4},{8,11},{9,10},{10,... | collective-permute-start | bytes 344072 | tf_op jit(solution)/shard_map/ppermute | solution.py:19
  91.0 5.1 %collective-permute-start.43 = (bf16[2,56,512]{2,1,0:T(8,128)(2,1)S(1)}, bf16[2,56,512]{2,1,0:T(8,128)(2,1)S(1)}, u32[]{:S(2)}, u32[]{:S(2)}) collective-permute-start(bf16[2,56,512]{2,1,0:T(8,128)(2,1)S(1)} %get-tuple-element.28), channel_id=1, source_target_pairs={{0,2},{1,3},{2,0},{3,1},{4,6},{5,7},{6,4},{7,5},{8,10},{9,11},{10,... | collective-permute-start | bytes 344072 | tf_op jit(solution)/shard_map/ppermute | solution.py:19
  (2 other events, 3.3 us)
